TPU v7x, 128 devices: a whole 4x4x4 slice. The times are simulated.
128 devices in a mesh: lat: 8 (over y, core), lon: 16 (over z, x).
Axes of the slice: x: 4, y: 4, z: 4, core: 2. Of those that a mesh axis runs over, the one named last changes fastest.
Arguments:
- coarse: bfloat16 [122880, 1104], P(('lat', 'lon')), may hold values from -6 to 6
- w_mix: bfloat16 [69, 64], replicated, may hold values from -0.75 to 0.75
- interp: bfloat16 [16, 256], replicated, may hold values from -1.5 to 1.5
- kernel: bfloat16 [3, 3, 64, 64], replicated, may hold values from -0.25 to 0.25
- bias: float32 [64], replicated, may hold values from -3 to 3
- block_ids: int32 [128, 144], replicated, may hold values from 0 to 122879, as said below
- valid: int32 [128, 144], replicated, may hold values from 0 to 1, as said below
Outputs:
- fine_out: bfloat16 [64, 2304, 2048], P(None, 'lat', 'lon')
Inputs may be any that keep to these rules, and one draw needn't show every extreme that they name: `block_ids`: the coarse grid has 192 block rows and 640 block columns, held block-cyclically: block (r, c) is row ((r mod 8) * 16 + c mod 16) * 960 + (r div 8) * 40 + c div 16 of coarse. Slot p of tile t holds block (r0 + (t div 16) * 18 + p div 8, (c0 + (t mod 16) * 8 + p mod 8) mod (640)), with offsets r0 and c0 common to all tiles. Among the valid slots of one tile at most 3 name blocks of one device, and in every tile exactly 3 valid slots name blocks of some one device. Every tile has 3 or more valid slots.
All inputs are finite; a program needn't handle non-finite values.
Results may differ from a plain program's by a relative error of at most 0.0055.
Values may be sent and summed in bfloat16 or wider, within the bound.
A program may use at most 192 MiB of HBM per device.

v0:
```python
import jax
import jax.numpy as jnp
from jax import lax
from jax.sharding import PartitionSpec as P

PR = 18
PC = 8


def with_halo(block, sides, width):
    for axis, dim in sides:
        count = lax.axis_size(axis)
        forward = [(i, i + 1) for i in range(count - 1)]
        backward = [(target, source) for source, target in forward]
        low = lax.ppermute(
            lax.slice_in_dim(block, block.shape[dim] - width, None, axis=dim), axis, forward
        )
        high = lax.ppermute(lax.slice_in_dim(block, 0, width, axis=dim), axis, backward)
        block = jnp.concatenate([low, block, high], axis=dim)
    return block


def mix_rows(rows, w_mix):
    count = rows.shape[0]
    flat = rows.reshape(count * 16, w_mix.shape[0])
    mapped = jnp.dot(flat, w_mix, preferred_element_type=jnp.float32).astype(jnp.bfloat16)
    return mapped.reshape(count, 16 * w_mix.shape[1])


def slot_rank(owner, live):
    count = owner.shape[1]
    same = (owner[:, :, None] == owner[:, None, :]) & live[:, None, :]
    earlier = jnp.arange(count)[None, :] < jnp.arange(count)[:, None]
    return jnp.sum(same & earlier[None], axis=2)


def per_device(coarse, w_mix, interp, kernel, bias, block_ids, valid):
    n_lat = lax.axis_size("lat")
    n_lon = lax.axis_size("lon")
    n_dev = n_lat * n_lon
    most = (PR + n_lat - 1) // n_lat * ((PC + n_lon - 1) // n_lon)
    myself = lax.axis_index(("lat", "lon"))
    held = coarse.shape[0]
    channels = w_mix.shape[1]
    owner = block_ids // held
    local = block_ids % held
    live = valid > 0
    rank = slot_rank(owner, live)
    mine = live & (owner == myself)
    places = jnp.arange(most, dtype=jnp.int32)
    hits = mine[:, None, :] & (rank[:, None, :] == places[None, :, None])
    found = jnp.sum(jnp.where(hits, local[:, None, :], 0), axis=2)
    table = jnp.where(jnp.any(hits, axis=2), found, held)
    stacked = jnp.concatenate([coarse, jnp.zeros((1, coarse.shape[1]), coarse.dtype)], axis=0)
    outgoing = stacked[table]
    incoming = lax.all_to_all(outgoing, ("lat", "lon"), split_axis=0, concat_axis=0, tiled=True)
    incoming = incoming.reshape(n_dev * most, coarse.shape[1])
    arrived = mix_rows(incoming, w_mix)
    own_owner = lax.dynamic_index_in_dim(owner, myself, 0, False)
    own_rank = lax.dynamic_index_in_dim(rank, myself, 0, False)
    own_live = lax.dynamic_index_in_dim(valid, myself, 0, False)
    where_from = jnp.where(own_live > 0, own_owner * most + own_rank, 0)
    picked = arrived[where_from].reshape(PR * PC, 16, channels)
    picked = picked * own_live[:, None, None].astype(jnp.bfloat16)
    height = 16 * PR
    breadth = 16 * PC
    left = (
        picked.reshape(PR, PC, 16, channels).transpose(3, 0, 1, 2).reshape(channels * PR, breadth)
    )
    same_col = (jnp.arange(PC)[:, None] == jnp.arange(PC)[None, :]).astype(jnp.bfloat16)
    cells = interp.reshape(16, 16, 16)
    spread = same_col[:, None, None, :, None] * cells[None, :, :, None, :]
    spread = spread.reshape(breadth, 16 * breadth)
    image = jnp.dot(left, spread, preferred_element_type=jnp.float32).astype(jnp.bfloat16)
    image = image.reshape(channels, height, breadth)
    padded = with_halo(image, (("lat", 1), ("lon", 2)), 1)
    total = jnp.zeros((channels, height, breadth), jnp.float32)
    for tap_row in range(3):
        for tap_col in range(3):
            window = padded[:, tap_row : tap_row + height, tap_col : tap_col + breadth]
            total = total + jnp.einsum(
                "oc,chw->ohw", kernel[tap_row, tap_col], window, preferred_element_type=jnp.float32
            )
    land = jnp.broadcast_to(
        own_live.astype(jnp.float32).reshape(PR, 1, PC, 1), (PR, 16, PC, 16)
    ).reshape(height, breadth)
    return ((total + bias[:, None, None]) * land[None]).astype(jnp.bfloat16)


def solution(mesh):
    placed = (P(("lat", "lon"), None), P(), P(), P(), P(), P(), P())
    return jax.shard_map(
        per_device, mesh=mesh, in_specs=placed, out_specs=P(None, "lat", "lon"), check_vma=False
    )
```

profile of v0, /device:TPU:40, one launch (start us, length us, event | category | flops | bytes accessed | tf_op | source)
XLA Modules:
  0.0 211.6 jit_solution(3933851844532241639)
XLA Ops:
  2.0 3.8 %convert_reduce_fusion = s32[128,144]{0,1:T(8,128)S(1)} fusion(s32[128,144]{0,1:T(8,128)S(1)} %get-tuple-element.7, pred[144,144]{1,0:T(8,128)(4,1)S(1)} %iota_compare_fusion.1, pred[128,144]{0,1:T(8,128)(4,1)S(1)} %get-tuple-element.6), kind=kLoop, calls=%fused_computation.10 | loop fusion | flops 13252608 | bytes 186624 | tf_op jit(solution)/shard_map/reduce_sum | solution.py:34
  7.3 1.8 concatenate.23
  9.2 2.2 %gather_fusion = bf16[384,1104]{1,0:T(8,128)(2,1)S(1)} fusion(bf16[961,1104]{1,0:T(8,128)(2,1)S(1)} %concatenate.23, s32[1024]{0:T(1024)S(1)} %get-tuple-element.13), kind=kCustom, calls=%fused_computation | custom fusion | bytes 1697280 | tf_op jit(solution)/shard_map/gather | solution.py:55
  12.7 10.5 %all-to-all-start = ((bf16[128,3,1104]{2,1,0:T(4,128)(2,1)}), bf16[128,3,1104]{2,1,0:T(4,128)(2,1)S(1)}, u32[]{:S(2)}, u32[]{:S(2)}) async-start(bf16[128,3,1104]{2,1,0:T(4,128)(2,1)} %reshape.155), calls=%async_computation | async-start | bytes 2359296 | tf_op jit(solution)/shard_map/all_to_all | solution.py:56
  24.4 2.4 %broadcast_multiply_fusion = bf16[8,16,16,8,16]{4,3,2,1,0:T(8,128)(2,1)} fusion(bf16[16,16,16]{2,1,0:T(8,128)(2,1)S(1)} %mul.67, bf16[8,8]{1,0:T(8,128)(2,1)S(1)} %fusion.44), kind=kLoop, calls=%fused_computation.35 | loop fusion | flops 262144 | bytes 532608 | tf_op jit(solution)/shard_map/mul | solution.py:72
  26.8 8.8 %mul.70 = bf16[128,2048]{1,0:T(8,128)(2,1)} reshape(bf16[8,16,16,8,16]{4,3,2,1,0:T(8,128)(2,1)} %broadcast_multiply_fusion) | data formatting | bytes 1048576 | tf_op jit(solution)/shard_map/mul | solution.py:72
  35.6 6.6 %all-to-all-done = bf16[128,3,1104]{2,1,0:T(4,128)(2,1)S(1)} async-done(((bf16[128,3,1104]{2,1,0:T(4,128)(2,1)}), bf16[128,3,1104]{2,1,0:T(4,128)(2,1)S(1)}, u32[]{:S(2)}, u32[]{:S(2)}) %all-to-all-start) | async-done | bytes 847904 | tf_op jit(solution)/shard_map/all_to_all | solution.py:56
  42.2 3.2 %reshape_reshape.3 = bf16[6144,69]{1,0:T(8,128)(2,1)S(1)} reshape(bf16[128,3,1104]{2,1,0:T(4,128)(2,1)S(1)} %all-to-all-done) | data formatting | bytes 1695744 | tf_op jit(solution)/shard_map/reshape;reshape | solution.py:25
  52.1 4.1 %reshape.152 = bf16[1152,128]{0,1:T(8,128)(2,1)S(1)} reshape(bf16[64,18,8,16]{1,0,3,2:T(8,128)(2,1)} %multiply_bitcast_fusion) | data formatting | bytes 589824 | tf_op jit(solution)/shard_map/reshape | solution.py:68
  56.2 3.6 %convolution_convert_fusion = bf16[1152,2048]{1,0:T(8,128)(2,1)} fusion(bf16[1152,128]{0,1:T(8,128)(2,1)S(1)} %reshape.152, bf16[128,2048]{1,0:T(8,128)(2,1)S(1)} %copy-done.7), kind=kOutput, calls=%fused_computation.12 | convolution fusion | flops 606339072 | bytes 5537792 | tf_op jit(solution)/shard_map/dot_general | solution.py:74
  59.8 8.3 %reshape.153 = bf16[64,288,128]{2,1,0:T(8,128)(2,1)} reshape(bf16[1152,2048]{1,0:T(8,128)(2,1)} %convolution_convert_fusion) | data formatting | bytes 9437184 | tf_op jit(solution)/shard_map/reshape | solution.py:75
  68.1 4.3 %copy.77 = bf16[64,288,128]{2,0,1:T(8,128)(2,1)S(1)} copy(bf16[64,288,128]{2,1,0:T(8,128)(2,1)} %reshape.153) | data formatting | bytes 9437184 | tf_op jit(solution)/shard_map/reshape | solution.py:75
  72.5 1.9 collective-permute-start
  74.4 3.9 %collective-permute-start.1 = (bf16[64,1,128]{2,0,1:T(8,128)(2,1)S(1)}, bf16[64,1,128]{2,0,1:T(8,128)(2,1)S(1)}, u32[]{:S(2)}, u32[]{:S(2)}) collective-permute-start(bf16[64,1,128]{2,0,1:T(8,128)(2,1)S(1)} %get-tuple-element.11), channel_id=1, source_target_pairs={{16,0},{32,16},{48,32},{64,48},{80,64},{96,80},{112,96},{17,1},{33... | collective-permute-start | bytes 49160 | tf_op jit(solution)/shard_map/ppermute | solution.py:18
  78.3 5.4 %fusion.29 = f32[288,128,64]{1,2,0:T(8,128)} fusion(bf16[3,3,64,64]{3,2,1,0:T(8,128)(2,1)S(1)} %copy-done.9, bf16[64,288,128]{2,1,0:T(8,128)(2,1)S(1)} %copy-done.5), kind=kOutput, calls=%fused_computation.57 | convolution fusion | flops 301989888 | bytes 14172160 | tf_op jit(solution)/shard_map/oc,chw->ohw/dot_general | solution.py:81
  83.7 2.1 %constant_dynamic-update-slice_fusion.1 = bf16[64,290,128]{2,0,1:T(8,128)(2,1)S(1)} fusion(bf16[64,290,128]{2,0,1:T(8,128)(2,1)S(1)} %constant_dynamic-update-slice_fusion.2, bf16[64,288,128]{2,1,0:T(8,128)(2,1)S(1)} %copy-done.5), kind=kLoop, calls=%fused_computation.73 | loop fusion | bytes 9437184
  85.8 6.2 %fusion.54 = (bf16[64,290,1]{2,0,1:T(8,128)(2,1)}, bf16[64,290,1]{2,0,1:T(8,128)(2,1)}) fusion(bf16[64,290,128]{2,0,1:T(8,128)(2,1)S(1)} %constant_dynamic-update-slice_fusion), kind=kLoop, calls=%fused_computation.90 | loop fusion | bytes 148480 | tf_op jit(solution)/shard_map/slice | solution.py:18
  92.0 5.8 %copy.83 = bf16[64,290,1]{1,0,2:T(8,128)(2,1)S(1)} copy(bf16[64,290,1]{2,0,1:T(8,128)(2,1)} %get-tuple-element.8) | data formatting | bytes 74240 | tf_op jit(solution)/shard_map/slice | solution.py:18
  97.8 5.8 %copy.80 = bf16[64,290,1]{1,0,2:T(8,128)(2,1)S(1)} copy(bf16[64,290,1]{2,0,1:T(8,128)(2,1)} %get-tuple-element.9) | data formatting | bytes 74240 | tf_op jit(solution)/shard_map/slice | solution.py:16
  103.6 2.8 %collective-permute-start.2 = (bf16[64,290,1]{1,0,2:T(8,128)(2,1)S(1)}, bf16[64,290,1]{1,0,2:T(8,128)(2,1)S(1)}, u32[]{:S(2)}, u32[]{:S(2)}) collective-permute-start(bf16[64,290,1]{1,0,2:T(8,128)(2,1)S(1)} %copy.80), channel_id=1, source_target_pairs={{0,1},{1,2},{2,3},{3,4},{4,5},{5,6},{6,7},{7,8},{8,9},{9,10},{10,1... | collective-permute-start | bytes 111368 | tf_op jit(solution)/shard_map/ppermute | solution.py:15
  106.5 5.4 %collective-permute-start.3 = (bf16[64,290,1]{1,0,2:T(8,128)(2,1)S(1)}, bf16[64,290,1]{1,0,2:T(8,128)(2,1)S(1)}, u32[]{:S(2)}, u32[]{:S(2)}) collective-permute-start(bf16[64,290,1]{1,0,2:T(8,128)(2,1)S(1)} %copy.83), channel_id=1, source_target_pairs={{1,0},{2,1},{3,2},{4,3},{5,4},{6,5},{7,6},{8,7},{9,8},{10,9},{11,1... | collective-permute-start | bytes 111368 | tf_op jit(solution)/shard_map/ppermute | solution.py:18
  111.9 7.3 %fusion.14 = f32[288,128,64]{1,2,0:T(8,128)} fusion(bf16[64,1,128]{2,0,1:T(8,128)(2,1)S(1)} %collective-permute-done.1, bf16[64,288,128]{2,0,1:T(8,128)(2,1)} %copy-done.6, bf16[3,3,64,64]{3,2,1,0:T(8,128)(2,1)S(1)} %copy-done.9), kind=kOutput, calls=%fused_computation.26 | convolution fusion | flops 311427072 | bytes 14188544 | tf_op jit(solution)/shard_map/oc,chw->ohw/dot_general | solution.py:81
  119.2 5.1 %fusion.18 = f32[288,128,64]{1,2,0:T(8,128)} fusion(bf16[64,288,128]{2,0,1:T(8,128)(2,1)S(1)} %bitcast.72, bf16[64,1,128]{2,0,1:T(8,128)(2,1)S(1)} %collective-permute-done, bf16[3,3,64,64]{3,2,1,0:T(8,128)(2,1)S(1)} %copy-done.9), kind=kOutput, calls=%fused_computation.32 | convolution fusion | flops 311427072 | bytes 14188544 | tf_op jit(solution)/shard_map/oc,chw->ohw/dot_general | solution.py:81
  124.3 6.5 %copy.81 = bf16[64,290,1]{2,0,1:T(8,128)(2,1)} copy(bf16[64,290,1]{1,0,2:T(8,128)(2,1)S(1)} %collective-permute-done.2) | data formatting | bytes 74240 | tf_op jit(solution)/shard_map/ppermute | solution.py:15
  130.8 9.9 %fusion.10 = f32[288,128,64]{1,2,0:T(8,128)} fusion(bf16[64,290,1]{2,0,1:T(8,128)(2,1)} %copy.81, bf16[64,290,128]{2,0,1:T(8,128)(2,1)} %copy-done.2, bf16[3,3,64,64]{3,2,1,0:T(8,128)(2,1)S(1)} %copy-done.9), kind=kOutput, calls=%fused_computation.21 | convolution fusion | flops 311427072 | bytes 14242048 | tf_op jit(solution)/shard_map/oc,chw->ohw/dot_general | solution.py:81
  140.8 5.0 %fusion.16 = f32[288,128,64]{1,2,0:T(8,128)} fusion(bf16[64,290,128]{2,0,1:T(8,128)(2,1)S(1)} %bitcast.68, bf16[64,290,1]{2,0,1:T(8,128)(2,1)S(1)} %copy-done.4, bf16[3,3,64,64]{3,2,1,0:T(8,128)(2,1)S(1)} %copy-done.9), kind=kOutput, calls=%fused_computation.29 | convolution fusion | flops 311427072 | bytes 18956288 | tf_op jit(solution)/shard_map/oc,chw->ohw/dot_general | solution.py:81
  145.7 4.8 %fusion.7 = f32[288,128,64]{1,2,0:T(8,128)} fusion(bf16[64,290,1]{2,0,1:T(8,128)(2,1)S(1)} %copy-done.4, bf16[64,290,128]{2,0,1:T(8,128)(2,1)S(1)} %bitcast.68, bf16[3,3,64,64]{3,2,1,0:T(8,128)(2,1)S(1)} %copy-done.9), kind=kOutput, calls=%fused_computation.19 | convolution fusion | flops 311427072 | bytes 18956288 | tf_op jit(solution)/shard_map/oc,chw->ohw/dot_general | solution.py:81
  150.6 6.1 %copy.84 = bf16[64,290,1]{2,0,1:T(8,128)(2,1)} copy(bf16[64,290,1]{1,0,2:T(8,128)(2,1)S(1)} %collective-permute-done.3) | data formatting | bytes 74240 | tf_op jit(solution)/shard_map/ppermute | solution.py:18
  156.7 10.6 %fusion.4 = f32[288,128,64]{1,2,0:T(8,128)} fusion(bf16[64,290,128]{2,0,1:T(8,128)(2,1)} %copy-done.2, bf16[64,290,1]{2,0,1:T(8,128)(2,1)} %copy.84, bf16[3,3,64,64]{3,2,1,0:T(8,128)(2,1)S(1)} %copy-done.9), kind=kOutput, calls=%fused_computation.17 | convolution fusion | flops 311427072 | bytes 14242048 | tf_op jit(solution)/shard_map/oc,chw->ohw/dot_general | solution.py:81
  167.3 5.5 %fusion.1 = f32[288,128,64]{1,2,0:T(8,128)} fusion(bf16[64,290,128]{2,0,1:T(8,128)(2,1)S(1)} %bitcast.70, bf16[64,290,1]{2,0,1:T(8,128)(2,1)S(1)} %copy-done.3, bf16[3,3,64,64]{3,2,1,0:T(8,128)(2,1)S(1)} %copy-done.9), kind=kOutput, calls=%fused_computation.15 | convolution fusion | flops 311427072 | bytes 18956288 | tf_op jit(solution)/shard_map/oc,chw->ohw/dot_general | solution.py:81
  172.7 31.1 %fusion.20 = bf16[64,288,128]{2,0,1:T(8,128)(2,1)} fusion(f32[288,128]{1,0:T(8,128)S(1)} %mul.71, f32[64]{0:T(128)S(1)} %copy-done.11, f32[288,128,64]{1,2,0:T(8,128)} %fusion.14, f32[288,128,64]{1,2,0:T(8,128)} %fusion.16, f32[288,128,64]{1,2,0:T(8,128)} %fusion.1, f32[288,128,64]{1,2,0:T(8,128)} %fusion.29, f32[288,128,64]{1,2,0:T(8,128)} %fusion.7, ...), kind=kOutput, calls=%fused_computation.34 | convolution fusion | flops 337379328 | bytes 85168896 | tf_op jit(solution)/shard_map/oc,chw->ohw/dot_general | solution.py:81
  203.8 7.6 %copy.87 = bf16[64,288,128]{2,1,0:T(8,128)(2,1)} copy(bf16[64,288,128]{2,0,1:T(8,128)(2,1)} %fusion.20) | data formatting | bytes 9437184 | tf_op jit(solution)/shard_map/convert_element_type | solution.py:87
  (74 shorter events, 12.8 us)
Async XLA Ops:
  0.0 45.5 %copy-start = (bf16[69,64]{0,1:T(8,128)(2,1)S(1)}, bf16[69,64]{0,1:T(8,128)(2,1)}, u32[]{:S(2)}) copy-start(bf16[69,64]{0,1:T(8,128)(2,1)} %param.8) | copy-start | bytes 26500
  9.1 14.0 %copy-start.8 = (s32[128,144]{0,1:T(8,128)S(1)}, s32[128,144]{0,1:T(8,128)}, u32[]{:S(2)}) copy-start(s32[128,144]{0,1:T(8,128)} %param.13) | copy-start | bytes 221188
  9.2 14.7 %copy-start.10 = (bf16[16,256]{1,0:T(8,128)(2,1)S(1)}, bf16[16,256]{1,0:T(8,128)(2,1)}, u32[]{:S(2)}) copy-start(bf16[16,256]{1,0:T(8,128)(2,1)} %param.9) | copy-start | bytes 24580
  12.7 29.6 %all-to-all-start = ((bf16[128,3,1104]{2,1,0:T(4,128)(2,1)}), bf16[128,3,1104]{2,1,0:T(4,128)(2,1)S(1)}, u32[]{:S(2)}, u32[]{:S(2)}) async-start(bf16[128,3,1104]{2,1,0:T(4,128)(2,1)} %reshape.155), calls=%async_computation | async-start | bytes 2359296 | tf_op jit(solution)/shard_map/all_to_all | solution.py:56
  49.4 6.8 %copy-start.7 = (bf16[128,2048]{1,0:T(8,128)(2,1)S(1)}, bf16[128,2048]{1,0:T(8,128)(2,1)}, u32[]{:S(2)}) copy-start(bf16[128,2048]{1,0:T(8,128)(2,1)} %mul.70) | copy-start | bytes 1572868
  68.1 10.1 %copy-start.5 = (bf16[64,288,128]{2,1,0:T(8,128)(2,1)S(1)}, bf16[64,288,128]{2,1,0:T(8,128)(2,1)}, u32[]{:S(2)}) copy-start(bf16[64,288,128]{2,1,0:T(8,128)(2,1)} %reshape.153) | copy-start | bytes 14155780
  68.1 10.1 %copy-start.9 = (bf16[3,3,64,64]{3,2,1,0:T(8,128)(2,1)S(1)}, bf16[3,3,64,64]{3,2,1,0:T(8,128)(2,1)}, u32[]{:S(2)}) copy-start(bf16[3,3,64,64]{3,2,1,0:T(8,128)(2,1)} %param.10) | copy-start | bytes 221188
  72.5 11.2 %copy-start.6 = (bf16[64,288,128]{2,0,1:T(8,128)(2,1)}, bf16[64,288,128]{2,0,1:T(8,128)(2,1)S(1)}, u32[]{:S(2)}) copy-start(bf16[64,288,128]{2,0,1:T(8,128)(2,1)S(1)} %copy.77) | copy-start | bytes 14155780
  72.5 11.2 %collective-permute-start = (bf16[64,1,128]{2,0,1:T(8,128)(2,1)S(1)}, bf16[64,1,128]{2,0,1:T(8,128)(2,1)S(1)}, u32[]{:S(2)}, u32[]{:S(2)}) collective-permute-start(bf16[64,1,128]{2,0,1:T(8,128)(2,1)S(1)} %get-tuple-element.10), channel_id=1, source_target_pairs={{0,16},{16,32},{32,48},{48,64},{64,80},{80,96},{96,112},{1,17},{17... | collective-permute-start | bytes 49160 | tf_op jit(solution)/shard_map/ppermute | solution.py:15
  74.4 11.4 %collective-permute-start.1 = (bf16[64,1,128]{2,0,1:T(8,128)(2,1)S(1)}, bf16[64,1,128]{2,0,1:T(8,128)(2,1)S(1)}, u32[]{:S(2)}, u32[]{:S(2)}) collective-permute-start(bf16[64,1,128]{2,0,1:T(8,128)(2,1)S(1)} %get-tuple-element.11), channel_id=1, source_target_pairs={{16,0},{32,16},{48,32},{64,48},{80,64},{96,80},{112,96},{17,1},{33... | collective-permute-start | bytes 49160 | tf_op jit(solution)/shard_map/ppermute | solution.py:18
  85.8 6.2 %copy-start.2 = (bf16[64,290,128]{2,0,1:T(8,128)(2,1)}, bf16[64,290,128]{2,0,1:T(8,128)(2,1)S(1)}, u32[]{:S(2)}) copy-start(bf16[64,290,128]{2,0,1:T(8,128)(2,1)S(1)} %constant_dynamic-update-slice_fusion) | copy-start | bytes 14254084
  97.8 21.5 %slice-start.4 = ((s8[4718592]{0:T(1024)(128)(4,1)}), s8[524288]{0:T(1024)(128)(4,1)S(1)}, s32[]{:S(2)}) async-start(s8[4718592]{0:T(1024)(128)(4,1)} %bitcast.71), calls=%async_computation.5 | async-start | bytes 1048576
  103.6 15.6 %slice-start.5 = ((s8[4718592]{0:T(1024)(128)(4,1)}), s8[4194304]{0:T(1024)(128)(4,1)S(1)}, s32[]{:S(2)}) async-start(s8[4718592]{0:T(1024)(128)(4,1)} %bitcast.71), calls=%async_computation.6 | async-start | bytes 8388608
  103.6 20.7 %collective-permute-start.2 = (bf16[64,290,1]{1,0,2:T(8,128)(2,1)S(1)}, bf16[64,290,1]{1,0,2:T(8,128)(2,1)S(1)}, u32[]{:S(2)}, u32[]{:S(2)}) collective-permute-start(bf16[64,290,1]{1,0,2:T(8,128)(2,1)S(1)} %copy.80), channel_id=1, source_target_pairs={{0,1},{1,2},{2,3},{3,4},{4,5},{5,6},{6,7},{7,8},{8,9},{9,10},{10,1... | collective-permute-start | bytes 111368 | tf_op jit(solution)/shard_map/ppermute | solution.py:15
  106.5 44.1 %collective-permute-start.3 = (bf16[64,290,1]{1,0,2:T(8,128)(2,1)S(1)}, bf16[64,290,1]{1,0,2:T(8,128)(2,1)S(1)}, u32[]{:S(2)}, u32[]{:S(2)}) collective-permute-start(bf16[64,290,1]{1,0,2:T(8,128)(2,1)S(1)} %copy.83), channel_id=1, source_target_pairs={{1,0},{2,1},{3,2},{4,3},{5,4},{6,5},{7,6},{8,7},{9,8},{10,9},{11,1... | collective-permute-start | bytes 111368 | tf_op jit(solution)/shard_map/ppermute | solution.py:18
  124.3 16.4 %slice-start = ((s8[4751360]{0:T(1024)(128)(4,1)}), s8[557056]{0:T(1024)(128)(4,1)S(1)}, s32[]{:S(2)}) async-start(s8[4751360]{0:T(1024)(128)(4,1)} %bitcast.67), calls=%async_computation.1 | async-start | bytes 1114112
  130.8 9.9 %slice-start.1 = ((s8[4751360]{0:T(1024)(128)(4,1)}), s8[4194304]{0:T(1024)(128)(4,1)S(1)}, s32[]{:S(2)}) async-start(s8[4751360]{0:T(1024)(128)(4,1)} %bitcast.67), calls=%async_computation.2 | async-start | bytes 8388608
  130.8 9.9 %copy-start.4 = (bf16[64,290,1]{2,0,1:T(8,128)(2,1)S(1)}, bf16[64,290,1]{2,0,1:T(8,128)(2,1)}, u32[]{:S(2)}) copy-start(bf16[64,290,1]{2,0,1:T(8,128)(2,1)} %copy.81) | copy-start | bytes 111364
  150.6 16.7 %slice-start.2 = ((s8[4751360]{0:T(1024)(128)(4,1)}), s8[557056]{0:T(1024)(128)(4,1)S(1)}, s32[]{:S(2)}) async-start(s8[4751360]{0:T(1024)(128)(4,1)} %bitcast.69), calls=%async_computation.3 | async-start | bytes 1114112
  156.7 10.6 %slice-start.3 = ((s8[4751360]{0:T(1024)(128)(4,1)}), s8[4194304]{0:T(1024)(128)(4,1)S(1)}, s32[]{:S(2)}) async-start(s8[4751360]{0:T(1024)(128)(4,1)} %bitcast.69), calls=%async_computation.4 | async-start | bytes 8388608
  156.7 10.6 %copy-start.3 = (bf16[64,290,1]{2,0,1:T(8,128)(2,1)S(1)}, bf16[64,290,1]{2,0,1:T(8,128)(2,1)}, u32[]{:S(2)}) copy-start(bf16[64,290,1]{2,0,1:T(8,128)(2,1)} %copy.84) | copy-start | bytes 111364
  167.3 5.5 %copy-start.11 = (f32[64]{0:T(128)S(1)}, f32[64]{0:T(128)}, u32[]{:S(2)}) copy-start(f32[64]{0:T(128)} %param.11) | copy-start | bytes 772
  172.7 38.6 %copy-start.1 = (bf16[69,64]{0,1:T(8,128)(2,1)S(1)}, bf16[69,64]{0,1:T(8,128)(2,1)}, u32[]{:S(2)}) copy-start(bf16[69,64]{0,1:T(8,128)(2,1)} %param.8) | copy-start | bytes 26500
where the time goes:
time: 215 us; the launch traced here: 212 us
  matrix products  88.8 us (41%)
  local copies, waits for them, and re-layouts  79.9 us (37%)
  starting transfers between devices  24.5 us (11%)
  other arithmetic  11.2 us (5%)
  waiting for transfers between devices  6.63 us (3%)
    dot_general x9, matrix products, per_device(): jnp.einsum('oc,chw->ohw', kernel[tap_row, tap_col], window, preferred_ele...  84.6 us
    reshape x2, local copies, waits for them, and re-layouts, per_device(): image = image.reshape(channels, height, breadth)  12.6 us
    slice x2, local copies, waits for them, and re-layouts, with_halo(): lax.slice_in_dim(block, 0, width, axis=dim)  11.9 us
    all_to_all x1, starting transfers between devices, per_device(): lax.all_to_all(outgoing, ('lat', 'lon'), split_axis=0, concat_axis=0, til...  10.5 us
    ppermute x2, starting transfers between devices, with_halo(): lax.ppermute(lax.slice_in_dim(block, 0, width, axis=dim), axis, backward)  9.22 us
    mul x2, local copies, waits for them, and re-layouts, per_device(): spread = same_col[:, None, None, :, None] * cells[None, :, :, None, :]  8.92 us
    convert_element_type x1, local copies, waits for them, and re-layouts, per_device(): return ((total + bias[:, None, None]) * land[None]).astype(jnp.bfloat16)  7.56 us
    all_to_all x1, waiting for transfers between devices, per_device(): lax.all_to_all(outgoing, ('lat', 'lon'), split_axis=0, concat_axis=0, til...  6.62 us
  transfers between devices with their start and end apart: 5, of which 1 were waited for; matrix products, arithmetic and copies ran while one was open for 28% of the time, Pallas kernels for 0%

commit v1 on v0

v1 whole, which is shorter than its diff:
```python
import jax
import jax.numpy as jnp
from jax import lax
from jax.experimental import pallas as pl
from jax.experimental.pallas import tpu as pltpu
from jax.sharding import PartitionSpec as P

N_LAT = 8
N_LON = 16
DEVICES = N_LAT * N_LON
PR = 18
PC = 8
HELD = 960
HELD_COLS = 40
C_IN = 69
C = 64
MOST = 3
GROUP = 3
STEPS = PR // GROUP
BF16 = jnp.bfloat16
F32 = jnp.float32


def position():
    return lax.axis_index("lat"), lax.axis_index("lon")


def offsets(ids_ref):
    first = ids_ref[0, 0]
    owner = first // HELD
    local = first - owner * HELD
    row = local // HELD_COLS
    col = local - row * HELD_COLS
    return row * 8 + owner // N_LON, col * 16 + owner % N_LON


def iota(shape, dim):
    return lax.broadcasted_iota(jnp.int32, shape, dim)


def build_weights(w_ref, wide):
    wide[...] = jnp.zeros(wide.shape, F32)
    w = w_ref[...].astype(F32)
    for g in range(8):
        wide[g, 10 * g : 10 * g + C_IN, 0:C] = w
        wide[g, 10 * g + C_IN : 10 * g + 2 * C_IN, C : 2 * C] = w


def pack_blocks(ids_ref, coarse_ref, w_ref, send, wide, rows):
    a, b = position()
    r0, c0 = offsets(ids_ref)
    build_weights(w_ref, wide)
    first_row = (a - r0) & 7
    local_row = (r0 + first_row) >> 3
    first_col = (b - c0) & 15
    local_col = (c0 + first_col) >> 4
    count = DEVICES * MOST
    slot = iota((count, 128), 0)
    tile = (slot * 21846) >> 16
    place = slot - 3 * tile
    n = ((PR * (tile >> 4) + 6 - first_row) >> 3) + place
    n = jnp.clip(n, 0, PR - 1)
    m = jnp.clip((PC * (tile & 15) + PC - first_col) >> 4, 0, 7)
    col = local_col + m
    col = jnp.where(col >= HELD_COLS, col - HELD_COLS, col)
    which = (local_row + n) * HELD_COLS + col
    lane = iota((count, 128), 1)
    picks = [jnp.where(which - 128 * k == lane, 1.0, 0.0).astype(BF16) for k in range(8)]
    pick = jnp.concatenate(picks, axis=1)[:, :HELD]
    taken = jnp.dot(pick, coarse_ref[...], preferred_element_type=F32).astype(BF16)
    for g in range(8):
        width = min(256, 16 * C_IN - 128 * g)
        part = taken[:, 128 * g : 128 * g + width]
        rows[pl.ds(g, count, stride=8), :] = jnp.dot(
            part, wide[g, :width, :].astype(BF16), preferred_element_type=F32
        )
    send[...] = rows[...].reshape(count, 8, 128).astype(BF16)


def build_spread(interp_ref, spread):
    row = iota((48, 16), 0)
    cell = 2 * (row & 7) + jnp.where(row < 32, row >> 4, (row >> 3) & 1)
    choose = jnp.where(cell == iota((48, 16), 1), 1.0, 0.0).astype(BF16)
    source = jnp.dot(choose, interp_ref[...], preferred_element_type=F32).astype(BF16)
    lane = iota((1, 256), 1)
    fine = iota((256, 256), 0)
    row_id = iota((48, 256), 0)

    def body(index, carry):
        t = index >> 2
        slot = index & 3
        fy = 8 * t + 4 * (lane >> 7) + ((lane >> 5) & 3)
        over = jnp.where(fy == 15 * t, 15 - 15 * t, -1)
        from_y = jnp.where(slot == 3, over, fy + slot - 1)
        inside = (from_y >= 0) & (from_y <= 15)
        for dx in range(3):
            from_x = (lane & 31) + (dx - 1)
            target = jnp.where(inside, from_y * 16 + (from_x & 15), -1)
            hit = jnp.where(fine == target, 1.0, 0.0).astype(BF16)
            value = jnp.dot(source, hit, preferred_element_type=F32)
            outer = (-1, 9, 2)[dx]
            patch = jnp.where(row_id < 32, (row_id >> 3) & 1, outer)
            value = jnp.where(patch == (from_x >> 4), value, 0.0)
            for q in range(4):
                for v in range(2):
                    half = value[:, 128 * v : 128 * v + 128]
                    if q:
                        half = pltpu.roll(half, 32 * q, 1)
                    half = half.astype(BF16)
                    lanes = pl.ds(128 * v, 128)
                    start = pl.multiple_of(slot * 128 + 32 * dx, 32)
                    spread[t, q, pl.ds(start, 32), lanes] = half[:32]
                    if dx != 1:
                        start = pl.multiple_of(slot * 128 + 96 + 8 * dx, 16)
                        spread[t, q, pl.ds(start, 16), lanes] = half[32:]
        return carry

    lax.fori_loop(0, 8, body, 0)


def build_taps(kernel_ref, taps):
    taps[...] = jnp.zeros(taps.shape, BF16)
    for dy in range(3):
        for dx in range(3):
            taps[64 * dy : 64 * dy + 64, 64 * dx : 64 * dx + 64] = kernel_ref[dy, dx]


def prepare_kernel(ids_ref, coarse_ref, w_ref, interp_ref, kernel_ref, send, spread, taps, wide, rows):
    pack_blocks(ids_ref, coarse_ref, w_ref, send, wide, rows)
    build_spread(interp_ref, spread)
    build_taps(kernel_ref, taps)


def build_left(ids_ref, valid_ref, got, taps, left):
    lat, lon = position()
    r0, c0 = offsets(ids_ref)
    low = iota((8, 128), 1) < 64

    def body(row, carry):
        pr = row - 1
        u = PR * lat + pr
        holder = ((r0 + u) & 7) * N_LON
        start = (PR * lat + 6 - (u & 7)) >> 3
        place = (u >> 3) - start
        up = pr < 0
        down = pr >= PR
        near_lat = lat + jnp.where(up, -1, jnp.where(down, 1, 0))
        near_row = jnp.where(up, PR - 1, jnp.where(down, 0, pr))
        row_ok = (near_lat >= 0) & (near_lat < N_LAT)
        near_lat = jnp.clip(near_lat, 0, N_LAT - 1)
        blocks = []
        for col in range(PC + 2):
            pc = col - 1
            b = (c0 + PC * lon + pc) & 15
            near_lon = lon + (-1 if pc < 0 else 1 if pc >= PC else 0)
            ok = row_ok & (near_lon >= 0) & (near_lon < N_LON)
            near_lon = jnp.clip(near_lon, 0, N_LON - 1)
            live = valid_ref[near_lat * N_LON + near_lon, near_row * PC + pc % PC]
            live = jnp.where(ok, live, 0)
            block = got[(holder + b) * MOST + place].astype(F32)
            blocks.append(jnp.where(live > 0, block, 0.0))
        zero = jnp.zeros((8, 128), F32)
        keep = [jnp.where(low, x, 0.0) for x in blocks]
        keep_hi = [jnp.where(low, 0.0, x) for x in blocks]
        turned = [pltpu.roll(x, 64, 1) for x in keep_hi]
        turned_hi = [pltpu.roll(x, 64, 1) for x in keep]
        for pair in range(2):
            first, second = [], []
            for q in (2 * pair, 2 * pair + 1):
                j, k = 2 * q + 1, 2 * q + 2
                main = [keep[j], keep[k], turned[j], turned[k]]
                first += main
                first += [turned_hi[j], turned_hi[k], keep_hi[j], keep_hi[k]]
                first += [zero] * 4
                first += [keep[j - 1], turned[j - 1], zero, zero]
                second += [zero] * 8
                second += main
                second += [zero, zero, keep[k + 1], turned[k + 1]]
            right = jnp.concatenate(
                [
                    jnp.concatenate(first, axis=0).astype(BF16),
                    jnp.concatenate(second, axis=0).astype(BF16),
                ],
                axis=1,
            )
            value = lax.dot_general(
                taps[...], right, (((1,), (1,)), ((), ())), preferred_element_type=F32
            ).astype(BF16)
            start = pl.multiple_of(row * 64, 64)
            for side in range(2):
                for dy in range(3):
                    left[2 * pair + side, dy, pl.ds(start, 64), :] = value[
                        64 * dy : 64 * dy + 64, 128 * side : 128 * side + 128
                    ]
        return carry

    lax.fori_loop(0, PR + 2, body, 0)


def fine_kernel(ids_ref, valid_ref, got, spread, taps, bias_ref, out_ref, left, shift, stage):
    step = pl.program_id(0)

    @pl.when(step == 0)
    def _():
        build_left(ids_ref, valid_ref, got, taps, left)
        across = jnp.where(iota((64, 64), 0) == iota((64, 64), 1), bias_ref[...], 0.0)
        shift[...] = jnp.broadcast_to(jnp.sum(across, axis=1, keepdims=True), (64, 128))

    lat, lon = position()
    tile = lat * N_LON + lon
    size = GROUP * 64
    base = pl.multiple_of((GROUP * step + 1) * 64, 64)
    lane = iota((64, 128), 1) >> 4
    masks = []
    for r in range(GROUP):
        mask = jnp.zeros((64, 128), jnp.int32)
        for pc in range(PC):
            live = valid_ref[tile, (GROUP * step + r) * PC + pc]
            mask = jnp.where(lane == pc, live, mask)
        masks.append(mask > 0)
    land = jnp.concatenate(masks, axis=0)
    bias = jnp.concatenate([shift[...]] * GROUP, axis=0)
    quarter = iota((size, 128), 1) >> 5
    for t in range(2):
        parts = []
        for q in range(4):
            edge = left[q, 0, pl.ds(base - 64, size), :] if t == 0 else left[q, 2, pl.ds(base + 64, size), :]
            near = jnp.concatenate([left[q, 0, pl.ds(base, size), :], left[q, 1, pl.ds(base, size), :]], axis=1)
            far = jnp.concatenate([left[q, 2, pl.ds(base, size), :], edge], axis=1)
            parts.append(
                jnp.dot(near, spread[t, q, 0:256, :], preferred_element_type=F32)
                + jnp.dot(far, spread[t, q, 256:512, :], preferred_element_type=F32)
            )
        for v in range(2):
            for s in range(4):
                halves = [parts[(p - s) & 3][:, 128 * v : 128 * v + 128] for p in range(4)]
                value = jnp.where(quarter == 0, halves[0], jnp.where(quarter == 1, halves[1], jnp.where(quarter == 2, halves[2], halves[3])))
                if s:
                    value = pltpu.roll(value, 128 - 32 * s, 1)
                value = jnp.where(land, value + bias, 0.0)
                stage[pl.ds(8 * t + 4 * v + s, size, stride=16), :] = value
    for r in range(GROUP):
        block = stage[pl.ds(r * 1024, 1024), :].reshape(64, 16, 128)
        out_ref[:, 16 * r : 16 * r + 16, :] = block.astype(BF16)


def prepare(ids, coarse, w_mix, interp, kernel):
    vmem = pl.BlockSpec(memory_space=pltpu.VMEM)
    return pl.pallas_call(
        prepare_kernel,
        grid=(1,),
        out_shape=(
            jax.ShapeDtypeStruct((DEVICES * MOST, 8, 128), BF16),
            jax.ShapeDtypeStruct((2, 4, 512, 256), BF16),
            jax.ShapeDtypeStruct((192, 256), BF16),
        ),
        in_specs=[pl.BlockSpec((8, 128), lambda i: (0, 0), memory_space=pltpu.SMEM)] + [vmem] * 4,
        out_specs=(vmem, vmem, vmem),
        scratch_shapes=[
            pltpu.VMEM((8, 256, 128), F32),
            pltpu.VMEM((DEVICES * MOST * 8, 128), F32),
        ],
        name="prepare",
    )(ids, coarse, w_mix, interp, kernel)


def finish(ids, valid, got, spread, taps, bias):
    vmem = pl.BlockSpec(memory_space=pltpu.VMEM)
    return pl.pallas_call(
        fine_kernel,
        grid=(STEPS,),
        out_shape=jax.ShapeDtypeStruct((C, PR * 16, PC * 16), BF16),
        in_specs=[
            pl.BlockSpec((8, 128), lambda i: (0, 0), memory_space=pltpu.SMEM),
            pl.BlockSpec(memory_space=pltpu.SMEM),
            vmem,
            vmem,
            vmem,
            vmem,
        ],
        out_specs=pl.BlockSpec((C, GROUP * 16, PC * 16), lambda i: (0, i, 0)),
        scratch_shapes=[
            pltpu.VMEM((4, 3, (PR + 2) * 64, 128), BF16),
            pltpu.VMEM((64, 128), F32),
            pltpu.VMEM((GROUP * 64 * 16, 128), F32),
        ],
        name="finish",
    )(ids, valid, got, spread, taps, bias)


def per_device(coarse, w_mix, interp, kernel, bias, block_ids, valid):
    send, spread, taps = prepare(block_ids, coarse, w_mix, interp, kernel)
    got = lax.all_to_all(send, ("lat", "lon"), split_axis=0, concat_axis=0, tiled=True)
    return finish(block_ids, valid, got, spread, taps, bias.reshape(1, C))


def solution(mesh):
    placed = (P(("lat", "lon"), None), P(), P(), P(), P(), P(), P())
    return jax.shard_map(
        per_device, mesh=mesh, in_specs=placed, out_specs=P(None, "lat", "lon"), check_vma=False
    )
```

time: 215 us -> 57.8 us (0.27)
  the two profiles are of different devices: /device:TPU:40 before, /device:TPU:1 now
where the time goes in v1:
time: 57.8 us; the launch traced here: 57.5 us
  Pallas kernels  25.3 us (44%)
  waiting for transfers between devices  16 us (28%)
  starting transfers between devices  11.5 us (20%)
  local copies, waits for them, and re-layouts  4.74 us (8%)
    pallas_call x1, Pallas kernels, finish(): pl.pallas_call(fine_kernel, grid=(STEPS,), out_shape=jax.ShapeDtypeStruct...  18.1 us
    all_to_all x1, waiting for transfers between devices, per_device(): lax.all_to_all(send, ('lat', 'lon'), split_axis=0, concat_axis=0, tiled=T...  16 us
    all_to_all x1, starting transfers between devices, per_device(): lax.all_to_all(send, ('lat', 'lon'), split_axis=0, concat_axis=0, tiled=T...  11.5 us
    pallas_call x1, Pallas kernels, prepare(): pl.pallas_call(prepare_kernel, grid=(1,), out_shape=(jax.ShapeDtypeStruct...  7.24 us
    unnamed x7, local copies, waits for them, and re-layouts  4.74 us
  transfers between devices with their start and end apart: 1, of which 1 were waited for; matrix products, arithmetic and copies ran while one was open for 1% of the time, Pallas kernels for 0%

profile of v1, /device:TPU:1, one launch (start us, length us, event | category | flops | bytes accessed | tf_op | source)
XLA Modules:
  0.0 57.5 jit_solution(4428842715006287073)
XLA Ops:
  0.0 0.0 copy-start.1
  0.0 1.4 %copy.9.w_ref = bf16[69,64]{1,0:T(8,128)(2,1)} copy(bf16[69,64]{0,1:T(8,128)(2,1)} %param.8) | data formatting | bytes 17664 | tf_op args[1]
  1.4 1.6 %copy.10.ids_ref = s32[128,144]{1,0:T(8,128)} copy(s32[128,144]{0,1:T(8,128)} %param.12) | data formatting | bytes 147456 | tf_op args[5]
  3.1 7.2 %prepare.1 = (bf16[384,8,128]{2,1,0:T(8,128)(2,1)}, bf16[2,4,512,256]{3,2,1,0:T(8,128)(2,1)}, bf16[192,256]{1,0:T(8,128)(2,1)}) custom-call(s32[128,144]{1,0:T(8,128)} %copy.10.ids_ref, bf16[960,1104]{1,0:T(8,128)(2,1)} %coarse_ref.1, bf16[69,64]{1,0:T(8,128)(2,1)} %copy.9.w_ref, bf16[16,256]{1,0:T(8,128)(2,1)} %interp_ref.1, bf16[3,3,64,64]{3,2,1,0:T(8,128)(2,1)} %kernel_ref.1), custom_call_target="tpu_custom_call" | custom-call | tf_op jit(solution)/shard_map/prepare/pallas_call | solution.py:249
  10.3 11.5 %all-to-all-start = ((bf16[384,8,128]{2,1,0:T(8,128)(2,1)}), bf16[384,8,128]{2,1,0:T(8,128)(2,1)S(1)}, u32[]{:S(2)}, u32[]{:S(2)}) async-start(bf16[384,8,128]{2,1,0:T(8,128)(2,1)} %get-tuple-element.8), calls=%async_computation | async-start | bytes 1572864 | tf_op jit(solution)/shard_map/all_to_all | solution.py:293
  21.8 0.0 copy-done.1
  21.8 0.8 %copy.11.valid_ref = s32[128,144]{1,0:T(8,128)} copy(s32[128,144]{0,1:T(8,128)S(1)} %copy-done.1) | data formatting | bytes 147456 | tf_op args[6]
  22.6 16.0 %all-to-all-done.got = bf16[384,8,128]{2,1,0:T(8,128)(2,1)S(1)} async-done(((bf16[384,8,128]{2,1,0:T(8,128)(2,1)}), bf16[384,8,128]{2,1,0:T(8,128)(2,1)S(1)}, u32[]{:S(2)}, u32[]{:S(2)}) %all-to-all-start) | async-done | bytes 786464 | tf_op jit(solution)/shard_map/all_to_all | solution.py:293
  38.6 0.0 copy-start
  38.6 0.9 %copy-done = bf16[384,8,128]{2,1,0:T(8,128)(2,1)} copy-done((bf16[384,8,128]{2,1,0:T(8,128)(2,1)}, bf16[384,8,128]{2,1,0:T(8,128)(2,1)S(1)}, u32[]{:S(2)}) %copy-start) | copy-done | bytes 786456
  39.5 18.1 %finish.1 = bf16[64,288,128]{2,1,0:T(8,128)(2,1)} custom-call(s32[128,144]{1,0:T(8,128)} %copy.10.ids_ref, s32[128,144]{1,0:T(8,128)} %copy.11.valid_ref, bf16[384,8,128]{2,1,0:T(8,128)(2,1)} %copy-done, bf16[2,4,512,256]{3,2,1,0:T(8,128)(2,1)} %get-tuple-element.9.spread, bf16[192,256]{1,0:T(8,128)(2,1)} %get-tuple-element.10.taps, f32[1,64]{1,0:T(1,128)} %bitcast.1), custom_call_target="tpu_custom_call" | custom-call | tf_op jit(solution)/shard_map/finish/pallas_call | solution.py:269
Async XLA Ops:
  0.0 21.8 %copy-start.1 = (s32[128,144]{0,1:T(8,128)S(1)}, s32[128,144]{0,1:T(8,128)}, u32[]{:S(2)}) copy-start(s32[128,144]{0,1:T(8,128)} %param.13) | copy-start | bytes 221188
  10.3 28.2 %all-to-all-start = ((bf16[384,8,128]{2,1,0:T(8,128)(2,1)}), bf16[384,8,128]{2,1,0:T(8,128)(2,1)S(1)}, u32[]{:S(2)}, u32[]{:S(2)}) async-start(bf16[384,8,128]{2,1,0:T(8,128)(2,1)} %get-tuple-element.8), calls=%async_computation | async-start | bytes 1572864 | tf_op jit(solution)/shard_map/all_to_all | solution.py:293
  38.6 0.9 %copy-start = (bf16[384,8,128]{2,1,0:T(8,128)(2,1)}, bf16[384,8,128]{2,1,0:T(8,128)(2,1)S(1)}, u32[]{:S(2)}) copy-start(bf16[384,8,128]{2,1,0:T(8,128)(2,1)S(1)} %all-to-all-done.got) | copy-start | bytes 2359300

commit v2 on v1

--- a/solution.py
+++ b/solution.py
@@ -17,6 +17,7 @@
 MOST = 3
 GROUP = 3
 STEPS = PR // GROUP
+MESH = pl.DeviceIdType.MESH
 BF16 = jnp.bfloat16
 F32 = jnp.float32
 
@@ -40,7 +41,7 @@
 
 def build_weights(w_ref, wide):
     wide[...] = jnp.zeros(wide.shape, F32)
-    w = w_ref[...].astype(F32)
+    w = jnp.transpose(w_ref[...].astype(F32))
     for g in range(8):
         wide[g, 10 * g : 10 * g + C_IN, 0:C] = w
         wide[g, 10 * g + C_IN : 10 * g + 2 * C_IN, C : 2 * C] = w
@@ -74,7 +75,7 @@
         rows[pl.ds(g, count, stride=8), :] = jnp.dot(
             part, wide[g, :width, :].astype(BF16), preferred_element_type=F32
         )
-    send[...] = rows[...].reshape(count, 8, 128).astype(BF16)
+    send[...] = rows[...].reshape(DEVICES, MOST, 8, 128).astype(BF16)
 
 
 def build_spread(interp_ref, spread):
@@ -125,10 +126,45 @@
             taps[64 * dy : 64 * dy + 64, 64 * dx : 64 * dx + 64] = kernel_ref[dy, dx]
 
 
-def prepare_kernel(ids_ref, coarse_ref, w_ref, interp_ref, kernel_ref, send, spread, taps, wide, rows):
+def peer(me, k):
+    other = lax.rem(me + k, DEVICES)
+    return other, (lax.div(other, N_LON), lax.rem(other, N_LON))
+
+
+def exchange_kernel(
+    ids_ref, coarse_ref, w_ref, interp_ref, kernel_ref, got, spread, taps, wide, rows, send, send_sem, got_sem
+):
+    lat, lon = position()
+    me = lat * N_LON + lon
+    barrier = pltpu.get_barrier_semaphore()
+
+    def greet(k, carry):
+        pl.semaphore_signal(barrier, inc=1, device_id=peer(me, k)[1], device_id_type=MESH)
+        return carry
+
+    lax.fori_loop(1, DEVICES, greet, 0)
     pack_blocks(ids_ref, coarse_ref, w_ref, send, wide, rows)
+    pl.semaphore_wait(barrier, DEVICES - 1)
+
+    def push(k, carry):
+        other, where = peer(me, k)
+        pltpu.make_async_remote_copy(
+            src_ref=send.at[other],
+            dst_ref=got.at[me],
+            send_sem=send_sem,
+            recv_sem=got_sem,
+            device_id=where,
+            device_id_type=MESH,
+        ).start()
+        return carry
+
+    lax.fori_loop(1, DEVICES, push, 0)
+    got[me] = send[me]
     build_spread(interp_ref, spread)
     build_taps(kernel_ref, taps)
+    others = pl.ds(0, DEVICES - 1)
+    pltpu.make_async_copy(send.at[others], got.at[others], got_sem).wait()
+    pltpu.make_async_copy(send.at[others], got.at[others], send_sem).wait()
 
 
 def build_left(ids_ref, valid_ref, got, taps, left):
@@ -155,9 +191,9 @@
             near_lon = lon + (-1 if pc < 0 else 1 if pc >= PC else 0)
             ok = row_ok & (near_lon >= 0) & (near_lon < N_LON)
             near_lon = jnp.clip(near_lon, 0, N_LON - 1)
-            live = valid_ref[near_lat * N_LON + near_lon, near_row * PC + pc % PC]
+            live = valid_ref[near_row * PC + pc % PC, near_lat * N_LON + near_lon]
             live = jnp.where(ok, live, 0)
-            block = got[(holder + b) * MOST + place].astype(F32)
+            block = got[holder + b, place].astype(F32)
             blocks.append(jnp.where(live > 0, block, 0.0))
         zero = jnp.zeros((8, 128), F32)
         keep = [jnp.where(low, x, 0.0) for x in blocks]
@@ -215,7 +251,7 @@
     for r in range(GROUP):
         mask = jnp.zeros((64, 128), jnp.int32)
         for pc in range(PC):
-            live = valid_ref[tile, (GROUP * step + r) * PC + pc]
+            live = valid_ref[(GROUP * step + r) * PC + pc, tile]
             mask = jnp.where(lane == pc, live, mask)
         masks.append(mask > 0)
     land = jnp.concatenate(masks, axis=0)
@@ -244,13 +280,13 @@
         out_ref[:, 16 * r : 16 * r + 16, :] = block.astype(BF16)
 
 
-def prepare(ids, coarse, w_mix, interp, kernel):
+def exchange(ids, coarse, w_mix, interp, kernel):
     vmem = pl.BlockSpec(memory_space=pltpu.VMEM)
     return pl.pallas_call(
-        prepare_kernel,
+        exchange_kernel,
         grid=(1,),
         out_shape=(
-            jax.ShapeDtypeStruct((DEVICES * MOST, 8, 128), BF16),
+            jax.ShapeDtypeStruct((DEVICES, MOST, 8, 128), BF16),
             jax.ShapeDtypeStruct((2, 4, 512, 256), BF16),
             jax.ShapeDtypeStruct((192, 256), BF16),
         ),
@@ -259,8 +295,12 @@
         scratch_shapes=[
             pltpu.VMEM((8, 256, 128), F32),
             pltpu.VMEM((DEVICES * MOST * 8, 128), F32),
+            pltpu.VMEM((DEVICES, MOST, 8, 128), BF16),
+            pltpu.SemaphoreType.DMA,
+            pltpu.SemaphoreType.DMA,
         ],
-        name="prepare",
+        compiler_params=pltpu.CompilerParams(collective_id=0, has_side_effects=True),
+        name="exchange",
     )(ids, coarse, w_mix, interp, kernel)
 
 
@@ -289,9 +329,9 @@
 
 
 def per_device(coarse, w_mix, interp, kernel, bias, block_ids, valid):
-    send, spread, taps = prepare(block_ids, coarse, w_mix, interp, kernel)
-    got = lax.all_to_all(send, ("lat", "lon"), split_axis=0, concat_axis=0, tiled=True)
-    return finish(block_ids, valid, got, spread, taps, bias.reshape(1, C))
+    ids, live = block_ids.T, valid.T
+    got, spread, taps = exchange(ids, coarse, w_mix.T, interp, kernel)
+    return finish(ids, live, got, spread, taps, bias.reshape(1, C))
 
 
 def solution(mesh):

time: 57.8 us -> 43.8 us (0.76)
  Pallas kernels: 25.3 us -> 43.6 us
  waiting for transfers between devices: 16 us -> 0 us
  starting transfers between devices: 11.5 us -> 0 us
  local copies, waits for them, and re-layouts: 4.74 us -> 0 us
    pallas_call x1, Pallas kernels: 7.24 us -> 26.6 us  [exchange(): pl.pallas_call(exchange_kernel, grid=(1,), out_shape=(jax.ShapeDtypeStruc...]
    all_to_all x1 -> x0, waiting for transfers between devices: 16 us -> none  [per_device(): lax.all_to_all(send, ('lat', 'lon'), split_axis=0, concat_axis=0, tiled=T...]
    all_to_all x1 -> x0, starting transfers between devices: 11.5 us -> none  [per_device(): lax.all_to_all(send, ('lat', 'lon'), split_axis=0, concat_axis=0, tiled=T...]
    unnamed x7 -> x0, local copies, waits for them, and re-layouts: 4.74 us -> none
    pallas_call x1, Pallas kernels: 18.1 us -> 17 us  [finish(): pl.pallas_call(fine_kernel, grid=(STEPS,), out_shape=jax.ShapeDtypeStruct...]
  transfers between devices with their start and end apart: 1 -> 0, of which waited for: 1 -> 0; matrix products, arithmetic and copies ran while one was open for 1% -> 0% of each run, Pallas kernels for 0% -> 0%
where the time goes in v2:
time: 43.8 us; the launch traced here: 43.7 us
  Pallas kernels  43.6 us (100%)
    pallas_call x1, Pallas kernels, exchange(): pl.pallas_call(exchange_kernel, grid=(1,), out_shape=(jax.ShapeDtypeStruc...  26.6 us
    pallas_call x1, Pallas kernels, finish(): pl.pallas_call(fine_kernel, grid=(STEPS,), out_shape=jax.ShapeDtypeStruct...  17 us

profile of v2, /device:TPU:1, one launch (start us, length us, event | category | flops | bytes accessed | tf_op | source)
XLA Modules:
  0.0 43.7 jit_solution(10114650434413700941)
XLA Ops:
  0.0 26.6 %exchange.1 = (bf16[128,3,8,128]{3,2,1,0:T(8,128)(2,1)}, bf16[2,4,512,256]{3,2,1,0:T(8,128)(2,1)}, bf16[192,256]{1,0:T(8,128)(2,1)}) custom-call(s32[144,128]{1,0:T(8,128)} %bitcast.4, bf16[960,1104]{1,0:T(8,128)(2,1)} %coarse_ref.1, bf16[64,69]{1,0:T(8,128)(2,1)} %bitcast.7, bf16[16,256]{1,0:T(8,128)(2,1)} %interp_ref.1, bf16[3,3,64,64]{3,2,1,0:T(8,128)(2,1)} %kernel_ref.1), custom_call_target="tpu_custom_call" | custom-call | tf_op jit(solution)/shard_map/exchange/pallas_call | solution.py:285
  26.6 17.0 %finish.1 = bf16[64,288,128]{2,1,0:T(8,128)(2,1)} custom-call(s32[144,128]{1,0:T(8,128)} %bitcast.5, s32[144,128]{1,0:T(8,128)} %bitcast.6, bf16[128,3,8,128]{3,2,1,0:T(8,128)(2,1)} %get-tuple-element.8.got, bf16[2,4,512,256]{3,2,1,0:T(8,128)(2,1)} %get-tuple-element.9.spread, bf16[192,256]{1,0:T(8,128)(2,1)} %get-tuple-element.10.taps, f32[1,64]{1,0:T(1,128)} %bitcast.8), custom_call_target="tpu_custom_call" | custom-call | tf_op jit(solution)/shard_map/finish/pallas_call | solution.py:309

commit v3 on v1

v3 whole, which is shorter than its diff:
```python
import jax
import jax.numpy as jnp
from jax import lax
from jax.experimental import pallas as pl
from jax.experimental.pallas import tpu as pltpu
from jax.sharding import PartitionSpec as P

N_LAT = 8
N_LON = 16
DEVICES = N_LAT * N_LON
PR = 18
PC = 8
HELD = 960
HELD_COLS = 40
C_IN = 69
C = 64
MOST = 3
GROUP = 6
EARLY = 2 * 6 * 16
PITCH = GROUP * 64 + 8
PARTS = 1
BATCH = GROUP * PARTS
LEFT = (4, 3, (PR + 2) * 64, 128)
MESH = pl.DeviceIdType.MESH
BF16 = jnp.bfloat16
F32 = jnp.float32


def position():
    return lax.axis_index("lat"), lax.axis_index("lon")


def offsets(ids_ref):
    first = ids_ref[0, 0]
    owner = first // HELD
    local = first - owner * HELD
    row = local // HELD_COLS
    col = local - row * HELD_COLS
    return row * 8 + owner // N_LON, col * 16 + owner % N_LON


def iota(shape, dim):
    return lax.broadcasted_iota(jnp.int32, shape, dim)


def build_weights(w_ref, wide):
    wide[...] = jnp.zeros(wide.shape, F32)
    w = jnp.transpose(w_ref[...].astype(F32))
    for g in range(8):
        wide[g, 10 * g : 10 * g + C_IN, 0:C] = w
        wide[g, 10 * g + C_IN : 10 * g + 2 * C_IN, C : 2 * C] = w


def pack_blocks(ids_ref, coarse, wide, rows, send):
    a, b = position()
    r0, c0 = offsets(ids_ref)
    first_row = (a - r0) & 7
    local_row = (r0 + first_row) >> 3
    first_col = (b - c0) & 15
    local_col = (c0 + first_col) >> 4
    count = DEVICES * MOST
    slot = iota((count, 128), 0)
    tile = slot & (DEVICES - 1)
    n = ((PR * (tile >> 4) + 6 - first_row) >> 3) + (slot >> 7)
    n = jnp.clip(n, 0, PR - 1)
    m = jnp.clip((PC * (tile & 15) + PC - first_col) >> 4, 0, 7)
    col = local_col + m
    col = jnp.where(col >= HELD_COLS, col - HELD_COLS, col)
    which = (local_row + n) * HELD_COLS + col
    lane = iota((count, 128), 1)
    picks = [jnp.where(which - 128 * k == lane, 1.0, 0.0).astype(BF16) for k in range(8)]
    pick = jnp.concatenate(picks, axis=1)[:, :HELD]
    taken = jnp.dot(pick, coarse[...], preferred_element_type=F32).astype(BF16)
    for g in range(8):
        width = min(256, 16 * C_IN - 128 * g)
        part = taken[:, 128 * g : 128 * g + width]
        rows[pl.ds(g, count, stride=8), :] = jnp.dot(
            part, wide[g, :width, :].astype(BF16), preferred_element_type=F32
        )
    send[...] = rows[...].reshape(MOST, DEVICES, 8, 128).astype(BF16)


def build_spread(interp_ref, spread):
    row = iota((48, 16), 0)
    cell = 2 * (row & 7) + jnp.where(row < 32, row >> 4, (row >> 3) & 1)
    choose = jnp.where(cell == iota((48, 16), 1), 1.0, 0.0).astype(BF16)
    source = jnp.dot(choose, interp_ref[...], preferred_element_type=F32).astype(BF16)
    lane = iota((1, 256), 1)
    fine = iota((256, 256), 0)
    row_id = iota((48, 256), 0)

    def body(index, carry):
        t = index >> 2
        slot = index & 3
        fy = 8 * t + 4 * (lane >> 7) + ((lane >> 5) & 3)
        over = jnp.where(fy == 15 * t, 15 - 15 * t, -1)
        from_y = jnp.where(slot == 3, over, fy + slot - 1)
        inside = (from_y >= 0) & (from_y <= 15)
        for dx in range(3):
            from_x = (lane & 31) + (dx - 1)
            target = jnp.where(inside, from_y * 16 + (from_x & 15), -1)
            hit = jnp.where(fine == target, 1.0, 0.0).astype(BF16)
            value = jnp.dot(source, hit, preferred_element_type=F32)
            outer = (-1, 9, 2)[dx]
            patch = jnp.where(row_id < 32, (row_id >> 3) & 1, outer)
            value = jnp.where(patch == (from_x >> 4), value, 0.0)
            for q in range(4):
                for v in range(2):
                    half = value[:, 128 * v : 128 * v + 128]
                    if q:
                        half = pltpu.roll(half, 32 * q, 1)
                    half = half.astype(BF16)
                    lanes = pl.ds(128 * v, 128)
                    start = pl.multiple_of(slot * 128 + 32 * dx, 32)
                    spread[t, q, pl.ds(start, 32), lanes] = half[:32]
                    if dx != 1:
                        start = pl.multiple_of(slot * 128 + 96 + 8 * dx, 16)
                        spread[t, q, pl.ds(start, 16), lanes] = half[32:]
        return carry

    lax.fori_loop(0, 8, body, 0)


def build_taps(kernel_ref, taps):
    taps[...] = jnp.zeros(taps.shape, BF16)
    for dy in range(3):
        for dx in range(3):
            taps[64 * dy : 64 * dy + 64, 64 * dx : 64 * dx + 64] = kernel_ref[dy, dx]


def far_first():
    def hops(step):
        return sum(min(d, 4 - d) for d in step[:3])

    steps = [(y, z, x, c) for y in range(4) for z in range(4) for x in range(4) for c in range(2)]
    return sorted(steps[1:], key=hops, reverse=True)


def peers():
    lat, lon = position()
    ys = [lax.rem(lax.div(lat, 2) + d, 4) * 2 for d in range(4)]
    cs = [lax.rem(lat + d, 2) for d in range(2)]
    zs = [lax.rem(lax.div(lon, 4) + d, 4) * 4 for d in range(4)]
    xs = [lax.rem(lon + d, 4) for d in range(4)]
    return [(ys[y] + cs[c], zs[z] + xs[x]) for y, z, x, c in far_first()]


def build_left(ids_ref, valid_ref, got, taps, left, first_row, last_row):
    lat, lon = position()
    r0, c0 = offsets(ids_ref)
    low = iota((8, 128), 1) < 64

    def pair_of_rows(index, carry):
        one_row(first_row + 2 * index)
        one_row(first_row + 2 * index + 1)
        return carry

    def one_row(row):
        pr = row - 1
        u = PR * lat + pr
        holder = ((r0 + u) & 7) * N_LON
        up = pr < 0
        down = pr >= PR
        near_lat = lat + jnp.where(up, -1, jnp.where(down, 1, 0))
        near_row = jnp.where(up, PR - 1, jnp.where(down, 0, pr))
        row_ok = (near_lat >= 0) & (near_lat < N_LAT)
        near_lat = jnp.clip(near_lat, 0, N_LAT - 1)
        blocks = []
        for col in range(PC + 2):
            pc = col - 1
            b = (c0 + PC * lon + pc) & 15
            near_lon = lon + (-1 if pc < 0 else 1 if pc >= PC else 0)
            ok = row_ok & (near_lon >= 0) & (near_lon < N_LON)
            near_lon = jnp.clip(near_lon, 0, N_LON - 1)
            live = valid_ref[near_row * PC + pc % PC, near_lat * N_LON + near_lon]
            live = jnp.where(ok, live, 0)
            block = got[holder + b].astype(F32)
            blocks.append(jnp.where(live > 0, block, 0.0))
        zero = jnp.zeros((8, 128), F32)
        keep = [jnp.where(low, x, 0.0) for x in blocks]
        keep_hi = [jnp.where(low, 0.0, x) for x in blocks]
        turned = [pltpu.roll(x, 64, 1) for x in keep_hi]
        turned_hi = [pltpu.roll(x, 64, 1) for x in keep]
        for pair in range(2):
            first, second = [], []
            for q in (2 * pair, 2 * pair + 1):
                j, k = 2 * q + 1, 2 * q + 2
                main = [keep[j], keep[k], turned[j], turned[k]]
                first += main
                first += [turned_hi[j], turned_hi[k], keep_hi[j], keep_hi[k]]
                first += [zero] * 4
                first += [keep[j - 1], turned[j - 1], zero, zero]
                second += [zero] * 8
                second += main
                second += [zero, zero, keep[k + 1], turned[k + 1]]
            right = jnp.concatenate(
                [
                    jnp.concatenate(first, axis=0).astype(BF16),
                    jnp.concatenate(second, axis=0).astype(BF16),
                ],
                axis=1,
            )
            value = lax.dot_general(
                taps[...], right, (((1,), (1,)), ((), ())), preferred_element_type=F32
            ).astype(BF16)
            start = pl.multiple_of(row * 64, 64)
            for side in range(2):
                for dy in range(3):
                    left[2 * pair + side, dy, pl.ds(start, 64), :] = value[
                        64 * dy : 64 * dy + 64, 128 * side : 128 * side + 128
                    ]

    lax.fori_loop(0, (last_row - first_row) // 2, pair_of_rows, 0)


def build_shift(bias_ref, shift):
    across = jnp.where(iota((C, C), 0) == iota((C, C), 1), bias_ref[...], 0.0)
    shift[...] = jnp.broadcast_to(jnp.sum(across, axis=1, keepdims=True), (C, 128))


def build_land(valid_ref, land):
    lat, lon = position()
    tile = lat * N_LON + lon
    lane = iota((8, 128), 1) >> 4

    def body(row, carry):
        mask = jnp.zeros((8, 128), jnp.int32)
        for pc in range(PC):
            mask = jnp.where(lane == pc, valid_ref[row * PC + pc, tile], mask)
        land[row] = mask
        return carry

    lax.fori_loop(0, PR, body, 0)


def fine_rows(first, land, left, spread, shift, stages, out):
    size = GROUP * 64
    quarter = iota((size, 128), 1) >> 5
    bias = jnp.concatenate([shift[...]] * GROUP, axis=0)
    for part, stage in enumerate(stages):
        top = first + part * GROUP
        base = pl.multiple_of((top + 1) * 64, 64)
        keep = [jnp.concatenate([land[top + r]] * 8, axis=0) for r in range(GROUP)]
        keep = jnp.concatenate(keep, axis=0) > 0
        for t in range(2):
            parts = []
            for q in range(4):
                lhs = [left[q, dy, pl.ds(base, size), :] for dy in range(3)]
                if t == 0:
                    lhs.append(left[q, 0, pl.ds(base - 64, size), :])
                else:
                    lhs.append(left[q, 2, pl.ds(base + 64, size), :])
                lhs = jnp.concatenate(lhs, axis=1)
                parts.append(jnp.dot(lhs, spread[t, q], preferred_element_type=F32))
            for v in range(2):
                for s in range(4):
                    cut = [parts[(p - s) & 3][:, 128 * v : 128 * v + 128] for p in range(4)]
                    value = cut[3]
                    for p in (2, 1, 0):
                        value = jnp.where(quarter == p, cut[p], value)
                    if s:
                        value = pltpu.roll(value, 128 - 32 * s, 1)
                    value = jnp.where(keep, value + bias, 0.0)
                    stage[pl.ds((8 * t + 4 * v + s) * PITCH, size), :] = value
        for r in range(GROUP):
            for o in range(C):
                block = stage[pl.ds(64 * r + o, 16, stride=PITCH), :]
                row = 16 * (part * GROUP + r)
                out[o, row : row + 16, :] = block.astype(BF16)


def exchange_kernel(
    ids_ref, valid_ref, coarse_ref, w_ref, interp_ref, kernel_ref, bias_ref,
    left, spread, early, shift, land,
    coarse, wide, rows, send, got_first, got_next, got_last, taps, stage, load_sem, send_sem, got_sem,
):
    lat, lon = position()
    me = lat * N_LON + lon
    load = pltpu.make_async_copy(coarse_ref, coarse, load_sem)
    load.start()
    barrier = pltpu.get_barrier_semaphore()

    targets = peers()
    for where in targets:
        pl.semaphore_signal(barrier, inc=1, device_id=where, device_id_type=MESH)
    build_weights(w_ref, wide)
    build_taps(kernel_ref, taps)
    build_shift(bias_ref, shift)
    build_land(valid_ref, land)
    load.wait()
    pack_blocks(ids_ref, coarse, wide, rows, send)
    pl.semaphore_wait(barrier, DEVICES - 1)
    got = (got_first, got_next, got_last)
    for s in range(MOST):
        for where in targets:
            pltpu.make_async_remote_copy(
                src_ref=send.at[s, where[0] * N_LON + where[1]],
                dst_ref=got[s].at[me],
                send_sem=send_sem,
                recv_sem=got_sem.at[s],
                device_id=where,
                device_id_type=MESH,
            ).start()
        got[s][me] = send[s, me]
    build_spread(interp_ref, spread)
    others = pl.ds(0, DEVICES - 1)
    for s in range(MOST):
        pltpu.make_async_copy(send.at[s, others], got[s].at[others], got_sem.at[s]).wait()
        build_left(ids_ref, valid_ref, got[s], taps, left, 8 * s, min(8 * s + 8, PR + 2))
        if s < MOST - 1:
            rows_out = pl.ds(BATCH * 16 * s, BATCH * 16)
            stages = [stage.at[part] for part in range(PARTS)]
            fine_rows(BATCH * s, land, left, spread, shift, stages, early.at[:, rows_out, :])
    for s in range(MOST):
        pltpu.make_async_copy(send.at[s, others], got[s].at[others], send_sem).wait()


def finish_kernel(left, spread, early, shift, land, out, stage, late, early_sem, late_sem):
    head = pltpu.make_async_copy(early, out.at[:, pl.ds(0, EARLY), :], early_sem)
    head.start()
    tails = []
    for part in range(PARTS):
        first = 2 * BATCH + GROUP * part
        fine_rows(first, land, left, spread, shift, [stage.at[part]], late.at[part])
        where = pl.ds(16 * first, 16 * GROUP)
        tail = pltpu.make_async_copy(late.at[part], out.at[:, where, :], late_sem.at[part])
        tail.start()
        tails.append(tail)
    head.wait()
    for tail in tails:
        tail.wait()


def exchange(ids, valid, coarse, w_mix, interp, kernel, bias):
    vmem = pl.BlockSpec(memory_space=pltpu.VMEM)
    smem = pl.BlockSpec(memory_space=pltpu.SMEM)
    slots = (DEVICES, 8, 128)
    return pl.pallas_call(
        exchange_kernel,
        grid=(1,),
        out_shape=(
            pltpu.VMEM(LEFT, BF16),
            pltpu.VMEM((2, 4, 512, 256), BF16),
            pltpu.VMEM((C, EARLY, 128), BF16),
            pltpu.VMEM((C, 128), F32),
            pltpu.VMEM((PR, 8, 128), jnp.int32),
        ),
        in_specs=[
            pl.BlockSpec((8, 128), lambda i: (0, 0), memory_space=pltpu.SMEM),
            smem,
            pl.BlockSpec(memory_space=pl.ANY),
            vmem,
            vmem,
            vmem,
            vmem,
        ],
        out_specs=(vmem,) * 5,
        scratch_shapes=[
            pltpu.VMEM((HELD, 16 * C_IN), BF16),
            pltpu.VMEM((8, 256, 128), F32),
            pltpu.VMEM((DEVICES * MOST * 8, 128), F32),
            pltpu.VMEM((MOST,) + slots, BF16),
            pltpu.VMEM(slots, BF16),
            pltpu.VMEM(slots, BF16),
            pltpu.VMEM(slots, BF16),
            pltpu.VMEM((192, 256), BF16),
            pltpu.VMEM((PARTS, 16 * PITCH, 128), F32),
            pltpu.SemaphoreType.DMA,
            pltpu.SemaphoreType.DMA,
            pltpu.SemaphoreType.DMA((MOST,)),
        ],
        compiler_params=pltpu.CompilerParams(
            collective_id=0, has_side_effects=True, vmem_limit_bytes=54 * 2**20
        ),
        name="exchange",
    )(ids, valid, coarse, w_mix, interp, kernel, bias)


def finish(*arrays):
    vmem = pl.BlockSpec(memory_space=pltpu.VMEM)
    return pl.pallas_call(
        finish_kernel,
        grid=(1,),
        out_shape=jax.ShapeDtypeStruct((C, PR * 16, PC * 16), BF16),
        in_specs=[vmem] * 5,
        out_specs=pl.BlockSpec(memory_space=pl.ANY),
        scratch_shapes=[
            pltpu.VMEM((PARTS, 16 * PITCH, 128), F32),
            pltpu.VMEM((PARTS, C, GROUP * 16, 128), BF16),
            pltpu.SemaphoreType.DMA,
            pltpu.SemaphoreType.DMA((PARTS,)),
        ],
        compiler_params=pltpu.CompilerParams(vmem_limit_bytes=30 * 2**20),
        name="finish",
    )(*arrays)


def per_device(coarse, w_mix, interp, kernel, bias, block_ids, valid):
    stay = [block_ids.T, valid.T, bias.reshape(1, C)]
    ids, live, bias = [pltpu.with_memory_space_constraint(x, pltpu.HBM) for x in stay]
    arrived = exchange(ids, live, coarse, w_mix.T, interp, kernel, bias)
    return finish(*arrived)


def solution(mesh):
    placed = (P(("lat", "lon"), None), P(), P(), P(), P(), P(), P())
    return jax.shard_map(
        per_device, mesh=mesh, in_specs=placed, out_specs=P(None, "lat", "lon"), check_vma=False
    )
```

time: 57.8 us -> 30.1 us (0.52)
  waiting for transfers between devices: 16 us -> 0 us
  starting transfers between devices: 11.5 us -> 0 us
  local copies, waits for them, and re-layouts: 4.74 us -> 0 us
  Pallas kernels: 25.3 us -> 29.9 us
    all_to_all x1 -> x0, waiting for transfers between devices: 16 us -> none  [per_device(): lax.all_to_all(send, ('lat', 'lon'), split_axis=0, concat_axis=0, tiled=T...]
    all_to_all x1 -> x0, starting transfers between devices: 11.5 us -> none  [per_device(): lax.all_to_all(send, ('lat', 'lon'), split_axis=0, concat_axis=0, tiled=T...]
    unnamed x7 -> x0, local copies, waits for them, and re-layouts: 4.74 us -> none
    pallas_call x2, Pallas kernels: 25.3 us -> 29.9 us  [the longest x1 26.8 us: exchange(): pl.pallas_call(exchange_kernel, grid=(1,), out_shape=(pltpu.VMEM(LEFT, BF...]
  transfers between devices with their start and end apart: 1 -> 0, of which waited for: 1 -> 0; matrix products, arithmetic and copies ran while one was open for 1% -> 0% of each run, Pallas kernels for 0% -> 0%
where the time goes in v3:
time: 30.1 us; the launch traced here: 29.9 us
  Pallas kernels  29.9 us (99%)
    pallas_call x1, Pallas kernels, exchange(): pl.pallas_call(exchange_kernel, grid=(1,), out_shape=(pltpu.VMEM(LEFT, BF...  26.8 us
    pallas_call x1, Pallas kernels, finish(): pl.pallas_call(finish_kernel, grid=(1,), out_shape=jax.ShapeDtypeStruct((...  3.12 us

profile of v3, /device:TPU:1, one launch (start us, length us, event | category | flops | bytes accessed | tf_op | source)
XLA Modules:
  0.0 29.9 jit_solution(5694533020749581733)
XLA Ops:
  0.0 26.8 %exchange.1 = (bf16[4,3,1280,128]{3,2,1,0:T(8,128)(2,1)S(1)}, bf16[2,4,512,256]{3,2,1,0:T(8,128)(2,1)S(1)}, bf16[64,192,128]{2,1,0:T(8,128)(2,1)S(1)}, f32[64,128]{1,0:T(8,128)S(1)}, s32[18,8,128]{2,1,0:T(8,128)S(1)}) custom-call(s32[144,128]{1,0:T(8,128)} %bitcast.4, s32[144,128]{1,0:T(8,128)} %bitcast.5, bf16[960,1104]{1,0:T(8,128)(2,1)} %coarse_ref.1, ...), custom_call_target="tpu_custom_call" | custom-call | tf_op jit(solution)/shard_map/exchange/pallas_call | solution.py:338
  26.8 3.1 %finish.1 = bf16[64,288,128]{2,1,0:T(8,128)(2,1)} custom-call(bf16[4,3,1280,128]{3,2,1,0:T(8,128)(2,1)S(1)} %get-tuple-element.10.left, bf16[2,4,512,256]{3,2,1,0:T(8,128)(2,1)S(1)} %get-tuple-element.11.spread, bf16[64,192,128]{2,1,0:T(8,128)(2,1)S(1)} %get-tuple-element.12.early, f32[64,128]{1,0:T(8,128)S(1)} %get-tuple-element.13.shift, ...), custom_call_target="tpu_custom_call" | custom-call | tf_op jit(solution)/shard_map/finish/pallas_call | solution.py:381

commit v4 on v3

--- a/solution.py
+++ b/solution.py
@@ -19,6 +19,7 @@
 EARLY = 2 * 6 * 16
 PITCH = GROUP * 64 + 8
 PARTS = 1
+UNROLL = 4
 BATCH = GROUP * PARTS
 LEFT = (4, 3, (PR + 2) * 64, 128)
 MESH = pl.DeviceIdType.MESH
@@ -150,10 +151,6 @@
     r0, c0 = offsets(ids_ref)
     low = iota((8, 128), 1) < 64
 
-    def pair_of_rows(index, carry):
-        one_row(first_row + 2 * index)
-        one_row(first_row + 2 * index + 1)
-        return carry
 
     def one_row(row):
         pr = row - 1
@@ -203,14 +200,15 @@
             value = lax.dot_general(
                 taps[...], right, (((1,), (1,)), ((), ())), preferred_element_type=F32
             ).astype(BF16)
-            start = pl.multiple_of(row * 64, 64)
+            start = row * 64
             for side in range(2):
                 for dy in range(3):
                     left[2 * pair + side, dy, pl.ds(start, 64), :] = value[
                         64 * dy : 64 * dy + 64, 128 * side : 128 * side + 128
                     ]
 
-    lax.fori_loop(0, (last_row - first_row) // 2, pair_of_rows, 0)
+    for row in range(first_row, last_row):
+        one_row(row)
 
 
 def build_shift(bias_ref, shift):
@@ -233,15 +231,15 @@
     lax.fori_loop(0, PR, body, 0)
 
 
-def fine_rows(first, land, left, spread, shift, stages, out):
+def fine_rows(first, land, left, spread, shift, stages, out, done=None):
     size = GROUP * 64
     quarter = iota((size, 128), 1) >> 5
+    left_half, even_place = quarter < 2, (quarter & 1) == 0
     bias = jnp.concatenate([shift[...]] * GROUP, axis=0)
     for part, stage in enumerate(stages):
         top = first + part * GROUP
         base = pl.multiple_of((top + 1) * 64, 64)
-        keep = [jnp.concatenate([land[top + r]] * 8, axis=0) for r in range(GROUP)]
-        keep = jnp.concatenate(keep, axis=0) > 0
+        keep = [jnp.concatenate([land[top + r]] * 2, axis=0) > 0 for r in range(GROUP)]
         for t in range(2):
             parts = []
             for q in range(4):
@@ -253,41 +251,53 @@
                 lhs = jnp.concatenate(lhs, axis=1)
                 parts.append(jnp.dot(lhs, spread[t, q], preferred_element_type=F32))
             for v in range(2):
-                for s in range(4):
-                    cut = [parts[(p - s) & 3][:, 128 * v : 128 * v + 128] for p in range(4)]
-                    value = cut[3]
-                    for p in (2, 1, 0):
-                        value = jnp.where(quarter == p, cut[p], value)
+                cut = [part[:, 128 * v : 128 * v + 128] for part in parts]
+                even = [jnp.where(left_half, cut[k], cut[2 - k]) for k in (0, 2)]
+                odd = [jnp.where(left_half, cut[k], cut[4 - k]) for k in (1, 3)]
+                mixes = [(even[0], odd[0]), (odd[1], even[0]), (even[1], odd[1]), (odd[0], even[1])]
+                for s, (first_part, second_part) in enumerate(mixes):
+                    value = jnp.where(even_place, first_part, second_part)
                     if s:
                         value = pltpu.roll(value, 128 - 32 * s, 1)
-                    value = jnp.where(keep, value + bias, 0.0)
+                    value = value + bias
                     stage[pl.ds((8 * t + 4 * v + s) * PITCH, size), :] = value
         for r in range(GROUP):
             for o in range(C):
                 block = stage[pl.ds(64 * r + o, 16, stride=PITCH), :]
                 row = 16 * (part * GROUP + r)
-                out[o, row : row + 16, :] = block.astype(BF16)
+                out[o, row : row + 16, :] = jnp.where(keep[r], block, 0.0).astype(BF16)
+            if done is not None:
+                done(part * GROUP + r)
 
 
 def exchange_kernel(
-    ids_ref, valid_ref, coarse_ref, w_ref, interp_ref, kernel_ref, bias_ref,
+    ids_hbm, valid_hbm, coarse_hbm, w_hbm, interp_hbm, kernel_hbm, bias_hbm,
     left, spread, early, shift, land,
-    coarse, wide, rows, send, got_first, got_next, got_last, taps, stage, load_sem, send_sem, got_sem,
+    coarse, wide, rows, send, got_first, got_next, got_last, taps, stage,
+    ids_ref, valid_ref, w_ref, interp_ref, kernel_ref, bias_ref, load_sem, send_sem, got_sem,
 ):
     lat, lon = position()
     me = lat * N_LON + lon
-    load = pltpu.make_async_copy(coarse_ref, coarse, load_sem)
-    load.start()
+    sources = (
+        coarse_hbm, w_hbm, ids_hbm.at[pl.ds(0, 8), :], kernel_hbm, bias_hbm, valid_hbm, interp_hbm,
+    )
+    places = (coarse, w_ref, ids_ref, kernel_ref, bias_ref, valid_ref, interp_ref)
+    loads = [pltpu.make_async_copy(*pair, load_sem.at[k]) for k, pair in enumerate(zip(sources, places))]
+    for load in loads:
+        load.start()
     barrier = pltpu.get_barrier_semaphore()
 
     targets = peers()
     for where in targets:
         pl.semaphore_signal(barrier, inc=1, device_id=where, device_id_type=MESH)
+    loads[1].wait()
     build_weights(w_ref, wide)
+    for load in loads[2:]:
+        load.wait()
     build_taps(kernel_ref, taps)
     build_shift(bias_ref, shift)
     build_land(valid_ref, land)
-    load.wait()
+    loads[0].wait()
     pack_blocks(ids_ref, coarse, wide, rows, send)
     pl.semaphore_wait(barrier, DEVICES - 1)
     got = (got_first, got_next, got_last)
@@ -318,22 +328,21 @@
 def finish_kernel(left, spread, early, shift, land, out, stage, late, early_sem, late_sem):
     head = pltpu.make_async_copy(early, out.at[:, pl.ds(0, EARLY), :], early_sem)
     head.start()
-    tails = []
-    for part in range(PARTS):
-        first = 2 * BATCH + GROUP * part
-        fine_rows(first, land, left, spread, shift, [stage.at[part]], late.at[part])
-        where = pl.ds(16 * first, 16 * GROUP)
-        tail = pltpu.make_async_copy(late.at[part], out.at[:, where, :], late_sem.at[part])
-        tail.start()
-        tails.append(tail)
+    first = 2 * BATCH
+
+    def copy(r):
+        rows_out = pl.ds(16 * (first + r), 16)
+        return pltpu.make_async_copy(late.at[:, pl.ds(16 * r, 16), :], out.at[:, rows_out, :], late_sem.at[r])
+
+    stages = [stage.at[part] for part in range(PARTS)]
+    fine_rows(first, land, left, spread, shift, stages, late, lambda r: copy(r).start())
     head.wait()
-    for tail in tails:
-        tail.wait()
+    for r in range(BATCH):
+        copy(r).wait()
 
 
 def exchange(ids, valid, coarse, w_mix, interp, kernel, bias):
     vmem = pl.BlockSpec(memory_space=pltpu.VMEM)
-    smem = pl.BlockSpec(memory_space=pltpu.SMEM)
     slots = (DEVICES, 8, 128)
     return pl.pallas_call(
         exchange_kernel,
@@ -345,15 +354,7 @@
             pltpu.VMEM((C, 128), F32),
             pltpu.VMEM((PR, 8, 128), jnp.int32),
         ),
-        in_specs=[
-            pl.BlockSpec((8, 128), lambda i: (0, 0), memory_space=pltpu.SMEM),
-            smem,
-            pl.BlockSpec(memory_space=pl.ANY),
-            vmem,
-            vmem,
-            vmem,
-            vmem,
-        ],
+        in_specs=[pl.BlockSpec(memory_space=pl.ANY)] * 7,
         out_specs=(vmem,) * 5,
         scratch_shapes=[
             pltpu.VMEM((HELD, 16 * C_IN), BF16),
@@ -365,7 +366,13 @@
             pltpu.VMEM(slots, BF16),
             pltpu.VMEM((192, 256), BF16),
             pltpu.VMEM((PARTS, 16 * PITCH, 128), F32),
-            pltpu.SemaphoreType.DMA,
+            pltpu.SMEM((8, 128), jnp.int32),
+            pltpu.SMEM((PR * PC, DEVICES), jnp.int32),
+            pltpu.VMEM((C, C_IN), BF16),
+            pltpu.VMEM((16, 256), BF16),
+            pltpu.VMEM((3, 3, C, C), BF16),
+            pltpu.VMEM((1, C), F32),
+            pltpu.SemaphoreType.DMA((7,)),
             pltpu.SemaphoreType.DMA,
             pltpu.SemaphoreType.DMA((MOST,)),
         ],
@@ -386,9 +393,9 @@
         out_specs=pl.BlockSpec(memory_space=pl.ANY),
         scratch_shapes=[
             pltpu.VMEM((PARTS, 16 * PITCH, 128), F32),
-            pltpu.VMEM((PARTS, C, GROUP * 16, 128), BF16),
+            pltpu.VMEM((C, BATCH * 16, 128), BF16),
             pltpu.SemaphoreType.DMA,
-            pltpu.SemaphoreType.DMA((PARTS,)),
+            pltpu.SemaphoreType.DMA((BATCH,)),
         ],
         compiler_params=pltpu.CompilerParams(vmem_limit_bytes=30 * 2**20),
         name="finish",
@@ -396,9 +403,7 @@
 
 
 def per_device(coarse, w_mix, interp, kernel, bias, block_ids, valid):
-    stay = [block_ids.T, valid.T, bias.reshape(1, C)]
-    ids, live, bias = [pltpu.with_memory_space_constraint(x, pltpu.HBM) for x in stay]
-    arrived = exchange(ids, live, coarse, w_mix.T, interp, kernel, bias)
+    arrived = exchange(block_ids.T, valid.T, coarse, w_mix.T, interp, kernel, bias.reshape(1, C))
     return finish(*arrived)
 
 

time: 30.1 us -> 25.7 us (0.85)
  Pallas kernels: 29.9 us -> 25.6 us
    pallas_call x1, Pallas kernels: 26.8 us -> 23.1 us  [exchange(): pl.pallas_call(exchange_kernel, grid=(1,), out_shape=(pltpu.VMEM(LEFT, BF...]
    pallas_call x1, Pallas kernels: 3.12 us -> 2.41 us  [finish(): pl.pallas_call(finish_kernel, grid=(1,), out_shape=jax.ShapeDtypeStruct((...]
where the time goes in v4:
time: 25.7 us; the launch traced here: 25.6 us
  Pallas kernels  25.6 us (100%)
    pallas_call x1, Pallas kernels, exchange(): pl.pallas_call(exchange_kernel, grid=(1,), out_shape=(pltpu.VMEM(LEFT, BF...  23.1 us
    pallas_call x1, Pallas kernels, finish(): pl.pallas_call(finish_kernel, grid=(1,), out_shape=jax.ShapeDtypeStruct((...  2.41 us

profile of v4, /device:TPU:1, one launch (start us, length us, event | category | flops | bytes accessed | tf_op | source)
XLA Modules:
  0.0 25.6 jit_solution(11984900601347276453)
XLA Ops:
  0.0 23.1 %exchange.1 = (bf16[4,3,1280,128]{3,2,1,0:T(8,128)(2,1)S(1)}, bf16[2,4,512,256]{3,2,1,0:T(8,128)(2,1)S(1)}, bf16[64,192,128]{2,1,0:T(8,128)(2,1)S(1)}, f32[64,128]{1,0:T(8,128)S(1)}, s32[18,8,128]{2,1,0:T(8,128)S(1)}) custom-call(s32[144,128]{1,0:T(8,128)} %bitcast.4, s32[144,128]{1,0:T(8,128)} %bitcast.5, bf16[960,1104]{1,0:T(8,128)(2,1)} %coarse_hbm.1, ...), custom_call_target="tpu_custom_call" | custom-call | tf_op jit(solution)/shard_map/exchange/pallas_call | solution.py:347
  23.2 2.4 %finish.1 = bf16[64,288,128]{2,1,0:T(8,128)(2,1)} custom-call(bf16[4,3,1280,128]{3,2,1,0:T(8,128)(2,1)S(1)} %get-tuple-element.10.left, bf16[2,4,512,256]{3,2,1,0:T(8,128)(2,1)S(1)} %get-tuple-element.11.spread, bf16[64,192,128]{2,1,0:T(8,128)(2,1)S(1)} %get-tuple-element.12.early, f32[64,128]{1,0:T(8,128)S(1)} %get-tuple-element.13.shift, ...), custom_call_target="tpu_custom_call" | custom-call | tf_op jit(solution)/shard_map/finish/pallas_call | solution.py:388

commit v5 on v4

--- a/solution.py
+++ b/solution.py
@@ -15,12 +15,10 @@
 C_IN = 69
 C = 64
 MOST = 3
-GROUP = 6
-EARLY = 2 * 6 * 16
-PITCH = GROUP * 64 + 8
-PARTS = 1
-UNROLL = 4
-BATCH = GROUP * PARTS
+PLAN = (((0, 6),), ((6, 4), (10, 4)))
+EARLY = 14 * 16
+PITCH = 8 * 64 + 4
+HEADS = 8
 LEFT = (4, 3, (PR + 2) * 64, 128)
 MESH = pl.DeviceIdType.MESH
 BF16 = jnp.bfloat16
@@ -231,43 +229,42 @@
     lax.fori_loop(0, PR, body, 0)
 
 
-def fine_rows(first, land, left, spread, shift, stages, out, done=None):
-    size = GROUP * 64
+def fine_rows(first, count, land, left, spread, shift, stage, out, done=None):
+    size = count * 64
+    pitch = size + 4
     quarter = iota((size, 128), 1) >> 5
     left_half, even_place = quarter < 2, (quarter & 1) == 0
-    bias = jnp.concatenate([shift[...]] * GROUP, axis=0)
-    for part, stage in enumerate(stages):
-        top = first + part * GROUP
-        base = pl.multiple_of((top + 1) * 64, 64)
-        keep = [jnp.concatenate([land[top + r]] * 2, axis=0) > 0 for r in range(GROUP)]
-        for t in range(2):
-            parts = []
-            for q in range(4):
-                lhs = [left[q, dy, pl.ds(base, size), :] for dy in range(3)]
-                if t == 0:
-                    lhs.append(left[q, 0, pl.ds(base - 64, size), :])
-                else:
-                    lhs.append(left[q, 2, pl.ds(base + 64, size), :])
-                lhs = jnp.concatenate(lhs, axis=1)
-                parts.append(jnp.dot(lhs, spread[t, q], preferred_element_type=F32))
-            for v in range(2):
-                cut = [part[:, 128 * v : 128 * v + 128] for part in parts]
-                even = [jnp.where(left_half, cut[k], cut[2 - k]) for k in (0, 2)]
-                odd = [jnp.where(left_half, cut[k], cut[4 - k]) for k in (1, 3)]
-                mixes = [(even[0], odd[0]), (odd[1], even[0]), (even[1], odd[1]), (odd[0], even[1])]
-                for s, (first_part, second_part) in enumerate(mixes):
-                    value = jnp.where(even_place, first_part, second_part)
-                    if s:
-                        value = pltpu.roll(value, 128 - 32 * s, 1)
-                    value = value + bias
-                    stage[pl.ds((8 * t + 4 * v + s) * PITCH, size), :] = value
-        for r in range(GROUP):
-            for o in range(C):
-                block = stage[pl.ds(64 * r + o, 16, stride=PITCH), :]
-                row = 16 * (part * GROUP + r)
-                out[o, row : row + 16, :] = jnp.where(keep[r], block, 0.0).astype(BF16)
-            if done is not None:
-                done(part * GROUP + r)
+    bias = jnp.concatenate([shift[...]] * count, axis=0)
+    base = (first + 1) * 64
+    keep = [jnp.concatenate([land[first + r]] * 2, axis=0) > 0 for r in range(count)]
+    for t in range(2):
+        parts = []
+        for q in range(4):
+            lhs = [left[q, dy, pl.ds(base, size), :] for dy in range(3)]
+            if t == 0:
+                lhs.append(left[q, 0, pl.ds(base - 64, size), :])
+            else:
+                lhs.append(left[q, 2, pl.ds(base + 64, size), :])
+            lhs = jnp.concatenate(lhs, axis=1)
+            parts.append(jnp.dot(lhs, spread[t, q], preferred_element_type=F32))
+        for v in range(2):
+            cut = [part[:, 128 * v : 128 * v + 128] for part in parts]
+            even = [jnp.where(left_half, cut[k], cut[2 - k]) for k in (0, 2)]
+            odd = [jnp.where(left_half, cut[k], cut[4 - k]) for k in (1, 3)]
+            mixes = [(even[0], odd[0]), (odd[1], even[0]), (even[1], odd[1]), (odd[0], even[1])]
+            for s, (first_part, second_part) in enumerate(mixes):
+                value = jnp.where(even_place, first_part, second_part)
+                if s:
+                    value = pltpu.roll(value, 128 - 32 * s, 1)
+                value = value + bias
+                stage[pl.ds((8 * t + 4 * v + s) * pitch, size), :] = value
+    for r in range(count):
+        for o in range(C):
+            block = stage[pl.ds(64 * r + o, 16, stride=pitch), :]
+            row = 16 * r
+            out[o, row : row + 16, :] = jnp.where(keep[r], block, 0.0).astype(BF16)
+        if done is not None:
+            done(r)
 
 
 def exchange_kernel(
@@ -318,26 +315,31 @@
         pltpu.make_async_copy(send.at[s, others], got[s].at[others], got_sem.at[s]).wait()
         build_left(ids_ref, valid_ref, got[s], taps, left, 8 * s, min(8 * s + 8, PR + 2))
         if s < MOST - 1:
-            rows_out = pl.ds(BATCH * 16 * s, BATCH * 16)
-            stages = [stage.at[part] for part in range(PARTS)]
-            fine_rows(BATCH * s, land, left, spread, shift, stages, early.at[:, rows_out, :])
+            for first, count in PLAN[s]:
+                rows_out = pl.ds(16 * first, 16 * count)
+                fine_rows(first, count, land, left, spread, shift, stage, early.at[:, rows_out, :])
     for s in range(MOST):
         pltpu.make_async_copy(send.at[s, others], got[s].at[others], send_sem).wait()
 
 
 def finish_kernel(left, spread, early, shift, land, out, stage, late, early_sem, late_sem):
-    head = pltpu.make_async_copy(early, out.at[:, pl.ds(0, EARLY), :], early_sem)
-    head.start()
-    first = 2 * BATCH
+    heads = []
+    for k in range(HEADS):
+        part = pl.ds(C // HEADS * k, C // HEADS)
+        there = out.at[part, pl.ds(0, EARLY), :]
+        heads.append(pltpu.make_async_copy(early.at[part], there, early_sem.at[k]))
+        heads[-1].start()
+    first = EARLY // 16
+    count = PR - first
 
     def copy(r):
         rows_out = pl.ds(16 * (first + r), 16)
         return pltpu.make_async_copy(late.at[:, pl.ds(16 * r, 16), :], out.at[:, rows_out, :], late_sem.at[r])
 
-    stages = [stage.at[part] for part in range(PARTS)]
-    fine_rows(first, land, left, spread, shift, stages, late, lambda r: copy(r).start())
-    head.wait()
-    for r in range(BATCH):
+    fine_rows(first, count, land, left, spread, shift, stage, late, lambda r: copy(r).start())
+    for head in heads:
+        head.wait()
+    for r in range(count):
         copy(r).wait()
 
 
@@ -365,7 +367,7 @@
             pltpu.VMEM(slots, BF16),
             pltpu.VMEM(slots, BF16),
             pltpu.VMEM((192, 256), BF16),
-            pltpu.VMEM((PARTS, 16 * PITCH, 128), F32),
+            pltpu.VMEM((16 * PITCH, 128), F32),
             pltpu.SMEM((8, 128), jnp.int32),
             pltpu.SMEM((PR * PC, DEVICES), jnp.int32),
             pltpu.VMEM((C, C_IN), BF16),
@@ -377,7 +379,7 @@
             pltpu.SemaphoreType.DMA((MOST,)),
         ],
         compiler_params=pltpu.CompilerParams(
-            collective_id=0, has_side_effects=True, vmem_limit_bytes=54 * 2**20
+            collective_id=0, has_side_effects=True, vmem_limit_bytes=53 * 2**20
         ),
         name="exchange",
     )(ids, valid, coarse, w_mix, interp, kernel, bias)
@@ -392,10 +394,10 @@
         in_specs=[vmem] * 5,
         out_specs=pl.BlockSpec(memory_space=pl.ANY),
         scratch_shapes=[
-            pltpu.VMEM((PARTS, 16 * PITCH, 128), F32),
-            pltpu.VMEM((C, BATCH * 16, 128), BF16),
-            pltpu.SemaphoreType.DMA,
-            pltpu.SemaphoreType.DMA((BATCH,)),
+            pltpu.VMEM((16 * PITCH, 128), F32),
+            pltpu.VMEM((C, PR * 16 - EARLY, 128), BF16),
+            pltpu.SemaphoreType.DMA((HEADS,)),
+            pltpu.SemaphoreType.DMA((PR - EARLY // 16,)),
         ],
         compiler_params=pltpu.CompilerParams(vmem_limit_bytes=30 * 2**20),
         name="finish",

time: 25.7 us -> 25.6 us (level)
  no operation moved by 1% of the time
where the time goes in v5:
time: 25.6 us; the launch traced here: 25.4 us
  Pallas kernels  25.4 us (99%)
    pallas_call x1, Pallas kernels, exchange(): pl.pallas_call(exchange_kernel, grid=(1,), out_shape=(pltpu.VMEM(LEFT, BF...  23.1 us
    pallas_call x1, Pallas kernels, finish(): pl.pallas_call(finish_kernel, grid=(1,), out_shape=jax.ShapeDtypeStruct((...  2.28 us

profile of v5, /device:TPU:1, one launch (start us, length us, event | category | flops | bytes accessed | tf_op | source)
XLA Modules:
  0.0 25.4 jit_solution(10756904382511621148)
XLA Ops:
  0.0 23.1 %exchange.1 = (bf16[4,3,1280,128]{3,2,1,0:T(8,128)(2,1)S(1)}, bf16[2,4,512,256]{3,2,1,0:T(8,128)(2,1)S(1)}, bf16[64,224,128]{2,1,0:T(8,128)(2,1)S(1)}, f32[64,128]{1,0:T(8,128)S(1)}, s32[18,8,128]{2,1,0:T(8,128)S(1)}) custom-call(s32[144,128]{1,0:T(8,128)} %bitcast.4, s32[144,128]{1,0:T(8,128)} %bitcast.5, bf16[960,1104]{1,0:T(8,128)(2,1)} %coarse_hbm.1, ...), custom_call_target="tpu_custom_call" | custom-call | tf_op jit(solution)/shard_map/exchange/pallas_call | solution.py:349
  23.2 2.3 %finish.1 = bf16[64,288,128]{2,1,0:T(8,128)(2,1)} custom-call(bf16[4,3,1280,128]{3,2,1,0:T(8,128)(2,1)S(1)} %get-tuple-element.10.left, bf16[2,4,512,256]{3,2,1,0:T(8,128)(2,1)S(1)} %get-tuple-element.11.spread, bf16[64,224,128]{2,1,0:T(8,128)(2,1)S(1)} %get-tuple-element.12.early, f32[64,128]{1,0:T(8,128)S(1)} %get-tuple-element.13.shift, ...), custom_call_target="tpu_custom_call" | custom-call | tf_op jit(solution)/shard_map/finish/pallas_call | solution.py:390

commit v6 on v5

--- a/solution.py
+++ b/solution.py
@@ -18,7 +18,7 @@
 PLAN = (((0, 6),), ((6, 4), (10, 4)))
 EARLY = 14 * 16
 PITCH = 8 * 64 + 4
-HEADS = 8
+HEADS = 4
 LEFT = (4, 3, (PR + 2) * 64, 128)
 MESH = pl.DeviceIdType.MESH
 BF16 = jnp.bfloat16

time: 25.6 us -> 25.5 us (level)
  no operation moved by 1% of the time
where the time goes in v6:
time: 25.5 us; the launch traced here: 25.4 us
  Pallas kernels  25.4 us (100%)
    pallas_call x1, Pallas kernels, exchange(): pl.pallas_call(exchange_kernel, grid=(1,), out_shape=(pltpu.VMEM(LEFT, BF...  23.1 us
    pallas_call x1, Pallas kernels, finish(): pl.pallas_call(finish_kernel, grid=(1,), out_shape=jax.ShapeDtypeStruct((...  2.25 us

profile of v6, /device:TPU:1, one launch (start us, length us, event | category | flops | bytes accessed | tf_op | source)
XLA Modules:
  0.0 25.4 jit_solution(3872602257799494515)
XLA Ops:
  0.0 23.1 %exchange.1 = (bf16[4,3,1280,128]{3,2,1,0:T(8,128)(2,1)S(1)}, bf16[2,4,512,256]{3,2,1,0:T(8,128)(2,1)S(1)}, bf16[64,224,128]{2,1,0:T(8,128)(2,1)S(1)}, f32[64,128]{1,0:T(8,128)S(1)}, s32[18,8,128]{2,1,0:T(8,128)S(1)}) custom-call(s32[144,128]{1,0:T(8,128)} %bitcast.4, s32[144,128]{1,0:T(8,128)} %bitcast.5, bf16[960,1104]{1,0:T(8,128)(2,1)} %coarse_hbm.1, ...), custom_call_target="tpu_custom_call" | custom-call | tf_op jit(solution)/shard_map/exchange/pallas_call | solution.py:349
  23.2 2.3 %finish.1 = bf16[64,288,128]{2,1,0:T(8,128)(2,1)} custom-call(bf16[4,3,1280,128]{3,2,1,0:T(8,128)(2,1)S(1)} %get-tuple-element.10.left, bf16[2,4,512,256]{3,2,1,0:T(8,128)(2,1)S(1)} %get-tuple-element.11.spread, bf16[64,224,128]{2,1,0:T(8,128)(2,1)S(1)} %get-tuple-element.12.early, f32[64,128]{1,0:T(8,128)S(1)} %get-tuple-element.13.shift, ...), custom_call_target="tpu_custom_call" | custom-call | tf_op jit(solution)/shard_map/finish/pallas_call | solution.py:390
